TPU v7x, 16 devices: a whole 2x2x2 slice. The times are simulated.
16 devices in a mesh: dp: 2 (over z), tp: 8 (over y, x, core).
Axes of the slice: x: 2, y: 2, z: 2, core: 2. Of those that a mesh axis runs over, the one named last changes fastest.
Arguments:
- hidden: bfloat16 [512, 3072], P('dp'), parts along dimension 0
- positions: int32 [512], P('dp'), parts along dimension 0
- k_cache: bfloat16 [2, 512, 128, 8, 128], P(None, 'dp', None, 'tp'), parts along dimension 1
- v_cache: bfloat16 [2, 512, 128, 8, 128], P(None, 'dp', None, 'tp'), parts along dimension 1
- attn_norm: bfloat16 [2, 3072], replicated
- w_query: bfloat16 [2, 3072, 3072], P(None, None, 'tp')
- w_key: bfloat16 [2, 3072, 1024], P(None, None, 'tp')
- w_value: bfloat16 [2, 3072, 1024], P(None, None, 'tp')
- w_out: bfloat16 [2, 3072, 3072], P(None, 'tp')
- mlp_norm: bfloat16 [2, 3072], replicated
- w_gate: bfloat16 [2, 3072, 8192], P(None, None, 'tp')
- w_up: bfloat16 [2, 3072, 8192], P(None, None, 'tp')
- w_down: bfloat16 [2, 8192, 3072], P(None, 'tp')
Outputs:
- output 1: bfloat16 [512, 3072], P('dp'), parts along dimension 0
- output 2: bfloat16 [2, 512, 128, 8, 128], P(None, 'dp', None, 'tp'), parts along dimension 1
- output 3: bfloat16 [2, 512, 128, 8, 128], P(None, 'dp', None, 'tp'), parts along dimension 1
There are 2 independent parts. A program takes and returns all parts, laid end to end along the dimension named above; an argument that names none is the same for every part.
All inputs are finite; a program needn't handle non-finite values.
Results may differ from a plain program's by a relative error of at most 0.02.
Values are sent between devices in bfloat16 or wider.
A program may use at most 1 GiB of HBM per device.

v0:
```python
import math
import jax
import jax.numpy as jnp
from jax import lax
from jax.sharding import PartitionSpec as P


def rms_norm(hidden, weight):
    hidden_f32 = hidden.astype(jnp.float32)
    mean_sq = jnp.mean(hidden_f32 * hidden_f32, axis=-1, keepdims=True)
    return (hidden_f32 * lax.rsqrt(mean_sq + 1e-5) * weight.astype(jnp.float32)).astype(jnp.bfloat16)


def rope_tables(positions, head_dim):
    half_dim = head_dim // 2
    inv_freq = jnp.power(500000.0, -jnp.arange(half_dim, dtype=jnp.float32) * (2.0 / head_dim))
    wavelen = (2.0 * math.pi) / inv_freq
    smooth = (8192.0 / wavelen - 1.0) / 3.0
    blended = (1.0 - smooth) * inv_freq / 8.0 + smooth * inv_freq
    scaled = jnp.where(wavelen < 2048.0, inv_freq, jnp.where(wavelen > 8192.0, inv_freq / 8.0, blended))
    angles = positions.astype(jnp.float32)[:, None] * scaled[None, :]
    return jnp.cos(angles), jnp.sin(angles)


def apply_rope(vectors, cos_tab, sin_tab):
    half_dim = vectors.shape[-1] // 2
    vec_f32 = vectors.astype(jnp.float32)
    first = vec_f32[..., :half_dim]
    second = vec_f32[..., half_dim:]
    cos_b = cos_tab[:, None, :]
    sin_b = sin_tab[:, None, :]
    return jnp.concatenate([first * cos_b - second * sin_b, second * cos_b + first * sin_b], axis=-1).astype(jnp.bfloat16)


def attend_split(query, k_old, v_old, key_new, value_new, before):
    score_scale = query.shape[-1] ** -0.5
    scores = jnp.einsum('bkgd,bskd->bkgs', query, k_old, preferred_element_type=jnp.float32) * score_scale
    scores = jnp.where(before, scores, -jnp.inf)
    score_new = jnp.einsum('clhe,cle->clh', query, key_new, preferred_element_type=jnp.float32) * score_scale
    row_peak = jnp.maximum(jnp.max(scores, axis=-1), score_new)
    weight_old = jnp.exp(scores - row_peak[..., None])
    weight_new = jnp.exp(score_new - row_peak)
    inv_total = 1.0 / (jnp.sum(weight_old, axis=-1) + weight_new)
    prob_old = (weight_old * inv_total[..., None]).astype(jnp.bfloat16)
    prob_new = (weight_new * inv_total).astype(jnp.bfloat16)
    attn_out = jnp.einsum('bkgs,bskd->bkgd', prob_old, v_old, preferred_element_type=jnp.float32)
    attn_out = attn_out + prob_new[..., None].astype(jnp.float32) * value_new[:, :, None, :].astype(jnp.float32)
    return attn_out.astype(jnp.bfloat16)


def attention_block(hidden, norm_weight, wq_layer, wk_layer, wv_layer, wo_layer, k_old, v_old, cos_tab, sin_tab, before):
    batch_size = hidden.shape[0]
    kv_heads = k_old.shape[2]
    head_dim = k_old.shape[3]
    q_heads = wq_layer.shape[1] // head_dim
    normed = rms_norm(hidden, norm_weight)
    query = jnp.dot(normed, wq_layer, preferred_element_type=jnp.float32).astype(jnp.bfloat16)
    key_new = jnp.dot(normed, wk_layer, preferred_element_type=jnp.float32).astype(jnp.bfloat16)
    value_new = jnp.dot(normed, wv_layer, preferred_element_type=jnp.float32).astype(jnp.bfloat16)
    query = apply_rope(query.reshape(batch_size, q_heads, head_dim), cos_tab, sin_tab)
    key_new = apply_rope(key_new.reshape(batch_size, kv_heads, head_dim), cos_tab, sin_tab)
    value_new = value_new.reshape(batch_size, kv_heads, head_dim)
    attended = attend_split(query.reshape(batch_size, kv_heads, q_heads // kv_heads, head_dim), k_old, v_old, key_new, value_new, before)
    mixed = jnp.dot(attended.reshape(batch_size, q_heads * head_dim), wo_layer, preferred_element_type=jnp.float32)
    return mixed.astype(jnp.bfloat16), key_new, value_new


def mlp_block(hidden, norm_weight, wg_layer, wu_layer, wd_layer):
    normed = rms_norm(hidden, norm_weight)
    gate_proj = jnp.dot(normed, wg_layer, preferred_element_type=jnp.float32).astype(jnp.bfloat16)
    up_proj = jnp.dot(normed, wu_layer, preferred_element_type=jnp.float32).astype(jnp.bfloat16)
    activated = (jax.nn.silu(gate_proj.astype(jnp.float32)) * up_proj.astype(jnp.float32)).astype(jnp.bfloat16)
    return jnp.dot(activated, wd_layer, preferred_element_type=jnp.float32).astype(jnp.bfloat16)


def write_rows(cache, rows, positions):
    at_pos = (jnp.arange(cache.shape[2])[None, :] == positions[:, None])[None, :, :, None, None]
    return jnp.where(at_pos, rows[:, :, None], cache)


def solution(mesh):
    row_spec = P('dp', None)
    pos_spec = P('dp')
    cache_spec = P(None, 'dp', None, 'tp', None)
    norm_spec = P(None, None)
    col_spec = P(None, None, 'tp')
    split_rows = P(None, 'tp', None)

    def local_step(hidden, positions, k_cache, v_cache, attn_norm, w_query, w_key, w_value, w_out, mlp_norm, w_gate, w_up, w_down):
        cos_tab, sin_tab = rope_tables(positions, k_cache.shape[4])
        before = (jnp.arange(k_cache.shape[2])[None, :] < positions[:, None])[:, None, None, :]
        k_rows = []
        v_rows = []
        for layer in range(k_cache.shape[0]):
            part_out, key_new, value_new = attention_block(hidden, attn_norm[layer], w_query[layer], w_key[layer], w_value[layer], w_out[layer], k_cache[layer], v_cache[layer], cos_tab, sin_tab, before)
            hidden = hidden + lax.psum(part_out, 'tp')
            part_out = mlp_block(hidden, mlp_norm[layer], w_gate[layer], w_up[layer], w_down[layer])
            hidden = hidden + lax.psum(part_out, 'tp')
            k_rows.append(key_new)
            v_rows.append(value_new)
        k_out = write_rows(k_cache, jnp.stack(k_rows), positions)
        v_out = write_rows(v_cache, jnp.stack(v_rows), positions)
        return hidden, k_out, v_out

    return jax.shard_map(local_step, mesh=mesh, in_specs=(row_spec, pos_spec, cache_spec, cache_spec, norm_spec, col_spec, col_spec, col_spec, split_rows, norm_spec, col_spec, col_spec, split_rows), out_specs=(row_spec, cache_spec, cache_spec), check_vma=False)
```

profile of v0, /device:TPU:0, one launch (start us, length us, event | category | flops | bytes accessed | tf_op | source)
XLA Modules:
  0.0 316.9 jit_solution(6299933611222931671)
XLA Ops:
  7.2 0.7 convert_element_type.198
  7.9 1.4 iota_compare_fusion
  9.3 1.9 fusion.28
  11.3 1.4 slice_convert_fusion.1
  12.7 0.5 multiply_cosine_fusion
  13.2 2.4 fusion.99
  15.6 0.3 fusion.145
  16.1 2.5 fusion.164
  18.5 2.7 fusion.95
  21.4 0.2 copy.87
  21.7 0.2 copy.86
  21.9 0.3 subtract_convert_fusion.1
  22.2 0.7 multiply_reduce_fusion.1
  22.9 8.0 %fusion.165 = (f32[256,3]{1,0:T(8,128)S(1)}, f32[256,3,128]{2,1,0:T(4,128)S(1)}) fusion(bf16[2,256,128,1,128]{4,2,1,3,0:T(8,128)(2,1)} %bitcast.158, bf16[256,3,64]{2,1,0:T(4,128)(2,1)S(1)} %get-tuple-element.12, bf16[256,3,64]{2,1,0:T(4,128)(2,1)S(1)} %get-tuple-element.11, pred[256,128]{1,0:T(8,128)(4,1)} %get-tuple-element.34), kind=kOutput, calls=%fused_computation.181 | convolution fusion | flops 25853184 | bytes 9014272 | tf_op jit(solution)/shard_map/bkgd,bskd->bkgs/dot_general | solution.py:37
  31.2 0.7 fusion.130
  32.2 4.8 %fusion.85 = bf16[256,3,128]{2,1,0:T(4,128)(2,1)S(1)} fusion(bf16[2,256,128,1,128]{4,2,1,3,0:T(8,128)(2,1)} %bitcast.156, f32[256,3,128]{2,1,0:T(4,128)S(1)} %get-tuple-element.38, f32[256,128]{1,0:T(8,128)} %get-tuple-element.35, f32[256,3]{1,0:T(8,128)S(1)} %copy.62, f32[256,3]{1,0:T(8,128)S(1)} %copy.60, f32[256,3]{1,0:T(8,128)S(1)} %copy.58), kind=kOutput, calls=%fused_computation.81 | convolution fusion | flops 25755648 | bytes 9118720 | tf_op jit(solution)/shard_map/bkgs,bskd->bkgd/dot_general | solution.py:46
  37.0 0.2 copy.63
  37.2 3.8 %convolution_convert_fusion.1 = bf16[256,3072]{1,0:T(8,128)(2,1)} fusion(bf16[256,384]{0,1:T(8,128)(2,1)S(1)} %bitcast.162, bf16[2,384,3072]{2,1,0:T(8,128)(2,1)} %param.21), kind=kOutput, calls=%fused_computation.39 | convolution fusion | flops 604766208 | bytes 4128768 | tf_op jit(solution)/shard_map/dot_general | solution.py:64
  41.1 0.2 all-reduce.7.cloned.1.call-start
  41.3 53.7 %all-reduce.5.cloned.1.call-done = bf16[256,3072]{1,0:T(8,128)(2,1)} async-done(((bf16[256,3072]{1,0:T(8,128)(2,1)}), bf16[256,3072]{1,0:T(8,128)(2,1)}) %all-reduce.5.cloned.1.call-update) | async-done | bytes 1572880 | tf_op jit(solution)/shard_map/psum | solution.py:96
  95.0 2.1 fusion.31
  97.1 4.6 %fusion.50 = bf16[256,1024]{1,0:T(8,128)(2,1)S(1)} fusion(bf16[2,3072,1024]{2,1,0:T(8,128)(2,1)} %param.23, bf16[256,3072]{1,0:T(8,128)(2,1)S(1)} %get-tuple-element.8, f32[3072]{0:T(1024)S(1)} %bitcast.182, f32[256]{0:T(256)S(1)} %add_rsqrt_fusion.2), kind=kOutput, calls=%fused_computation.66 | convolution fusion | flops 1614020608 | bytes 8401920 | tf_op jit(solution)/shard_map/dot_general | solution.py:70
  101.8 9.3 %fusion.22 = bf16[256,3072]{1,0:T(8,128)(2,1)} fusion(bf16[2,1024,3072]{2,1,0:T(8,128)(2,1)} %param.25, bf16[2,3072,1024]{2,1,0:T(8,128)(2,1)} %param.24, bf16[256,1024]{1,0:T(8,128)(2,1)S(1)} %fusion.50, bf16[256,3072]{1,0:T(8,128)(2,1)S(1)} %get-tuple-element.8, f32[3072]{0:T(1024)S(1)} %bitcast.183, f32[256]{0:T(256)S(1)} %add_rsqrt_fusion.2), kind=kOutput, calls=%fused_computation.36 | convolution fusion | flops 3227516928 | bytes 16266240 | tf_op jit(solution)/shard_map/dot_general | solution.py:73
  111.2 50.3 %all-reduce.7.cloned.1.call-done = bf16[256,3072]{1,0:T(8,128)(2,1)} async-done(((bf16[256,3072]{1,0:T(8,128)(2,1)}), bf16[256,3072]{1,0:T(8,128)(2,1)}) %all-reduce.7.cloned.1.call-update) | async-done | bytes 1572880 | tf_op jit(solution)/shard_map/psum | solution.py:98
  161.5 2.2 fusion.34
  163.7 2.0 fusion.101
  165.8 2.5 fusion.166
  168.2 1.1 fusion.92
  169.3 0.3 fusion.149
  169.7 0.6 copy-done.5
  170.4 0.2 copy.64
  170.6 0.2 copy.89
  170.8 0.2 copy.88
  171.1 0.3 subtract_convert_fusion
  171.3 7.9 %fusion.167 = (f32[256,3]{1,0:T(8,128)S(1)}, f32[256,3,128]{2,1,0:T(4,128)S(1)}) fusion(bf16[2,256,128,1,128]{4,2,1,3,0:T(8,128)(2,1)} %bitcast.159, bf16[256,3,64]{2,1,0:T(4,128)(2,1)S(1)} %get-tuple-element.10, bf16[256,3,64]{2,1,0:T(4,128)(2,1)S(1)} %get-tuple-element.9, pred[256,128]{1,0:T(8,128)(4,1)} %get-tuple-element.34), kind=kOutput, calls=%fused_computation.183 | convolution fusion | flops 25853184 | bytes 9014272 | tf_op jit(solution)/shard_map/bkgd,bskd->bkgs/dot_general | solution.py:37
  179.3 0.7 multiply_reduce_fusion
  180.3 0.7 fusion.131
  181.4 4.8 %fusion.84 = bf16[256,3,128]{2,1,0:T(4,128)(2,1)S(1)} fusion(bf16[2,256,128,1,128]{4,2,1,3,0:T(8,128)(2,1)} %bitcast.157, f32[256,3,128]{2,1,0:T(4,128)S(1)} %get-tuple-element.42, f32[256,128]{1,0:T(8,128)} %get-tuple-element.39, f32[256,3]{1,0:T(8,128)S(1)} %copy.73, f32[256,3]{1,0:T(8,128)S(1)} %copy.71, f32[256,3]{1,0:T(8,128)S(1)} %copy.69), kind=kOutput, calls=%fused_computation.80 | convolution fusion | flops 25755648 | bytes 9118720 | tf_op jit(solution)/shard_map/bkgs,bskd->bkgd/dot_general | solution.py:46
  186.2 0.2 copy.74
  186.4 3.9 %convolution_convert_fusion = bf16[256,3072]{1,0:T(8,128)(2,1)} fusion(bf16[256,384]{0,1:T(8,128)(2,1)S(1)} %bitcast.163, bf16[2,384,3072]{2,1,0:T(8,128)(2,1)} %param.21), kind=kOutput, calls=%fused_computation.38 | convolution fusion | flops 604766208 | bytes 4128768 | tf_op jit(solution)/shard_map/dot_general | solution.py:64
  190.3 0.3 all-reduce.11.cloned.1.call-start
  190.8 49.8 %all-reduce.9.cloned.1.call-done = bf16[256,3072]{1,0:T(8,128)(2,1)} async-done(((bf16[256,3072]{1,0:T(8,128)(2,1)}), bf16[256,3072]{1,0:T(8,128)(2,1)}) %all-reduce.9.cloned.1.call-update) | async-done | bytes 1572880 | tf_op jit(solution)/shard_map/psum | solution.py:96
  240.5 2.1 fusion.37
  242.7 4.6 %fusion.62 = bf16[256,1024]{1,0:T(8,128)(2,1)S(1)} fusion(bf16[2,3072,1024]{2,1,0:T(8,128)(2,1)} %param.23, bf16[256,3072]{1,0:T(8,128)(2,1)S(1)} %get-tuple-element.4, f32[3072]{0:T(1024)S(1)} %bitcast.174, f32[256]{0:T(256)S(1)} %add_rsqrt_fusion), kind=kOutput, calls=%fused_computation.70 | convolution fusion | flops 1614020608 | bytes 8401920 | tf_op jit(solution)/shard_map/dot_general | solution.py:70
  247.3 9.5 %fusion.25 = bf16[256,3072]{1,0:T(8,128)(2,1)} fusion(bf16[2,1024,3072]{2,1,0:T(8,128)(2,1)} %param.25, bf16[2,3072,1024]{2,1,0:T(8,128)(2,1)} %param.24, bf16[256,1024]{1,0:T(8,128)(2,1)S(1)} %fusion.62, bf16[256,3072]{1,0:T(8,128)(2,1)S(1)} %get-tuple-element.4, f32[3072]{0:T(1024)S(1)} %bitcast.175, f32[256]{0:T(256)S(1)} %add_rsqrt_fusion), kind=kOutput, calls=%fused_computation.37 | convolution fusion | flops 3227516928 | bytes 16266240 | tf_op jit(solution)/shard_map/dot_general | solution.py:73
  256.9 23.0 %broadcast_select_fusion = (bf16[2,256,128,1,128]{4,2,3,1,0:T(8,128)(2,1)}, bf16[2,256,128,1,128]{4,2,3,1,0:T(8,128)(2,1)}) fusion(bf16[2,256,128,1,128]{4,2,3,1,0:T(8,128)(2,1)} %param.16, pred[256,128]{1,0:T(8,128)(4,1)S(1)} %copy-done.9, bf16[2,256,128]{2,1,0:T(8,128)(2,1)S(1)} %maximum_bitcast_fusion.1, bf16[2,256,128,1,128]{4,2,3,1,0:T(8,128)(2,1)} %param.15, ...), kind=kLoop, calls=%fused_computation | loop fusion | flops 16777216 | bytes 67403776 | tf_op jit(solution)/shard_map/jit(_where)/select_n | solution.py:78
  279.9 27.3 %all-reduce.11.cloned.1.call-done = bf16[256,3072]{1,0:T(8,128)(2,1)} async-done(((bf16[256,3072]{1,0:T(8,128)(2,1)}), bf16[256,3072]{1,0:T(8,128)(2,1)}) %all-reduce.11.cloned.1.call-update) | async-done | bytes 1572880 | tf_op jit(solution)/shard_map/psum | solution.py:98
  307.2 3.1 add.119
  (74 shorter events, 2.2 us)
Async XLA Ops:
  7.2 87.8 %all-reduce.5.cloned.1.call-start = ((), (), s32[]{:S(2)}) async-start(), calls=%async_computation | async-start | bytes 3145728 | tf_op jit(solution)/shard_map/psum | solution.py:96
  7.2 8.7 %copy-start.14 = (f32[64]{0:T(128)}, f32[64]{0:T(128)S(1)}, u32[]{:S(2)}) copy-start(f32[64]{0:T(128)S(1)} %compare_select_fusion.1) | copy-start | bytes 772
  9.3 6.7 %copy-start = (bf16[256,3072]{1,0:T(8,128)(2,1)S(1)}, bf16[256,3072]{1,0:T(8,128)(2,1)}, u32[]{:S(2)}) copy-start(bf16[256,3072]{1,0:T(8,128)(2,1)} %param.13) | copy-start | bytes 4718596
  15.9 2.6 copy-start.1
  15.9 2.6 copy-start.3
  37.0 4.3 %copy-start.12 = (bf16[2,3072]{1,0:T(2,128)(2,1)S(1)}, bf16[2,3072]{1,0:T(2,128)(2,1)}, u32[]{:S(2)}) copy-start(bf16[2,3072]{1,0:T(2,128)(2,1)} %param.22) | copy-start | bytes 36868
  41.1 120.4 %all-reduce.7.cloned.1.call-start = ((), (), s32[]{:S(2)}) async-start(), calls=%async_computation.1 | async-start | bytes 3145728 | tf_op jit(solution)/shard_map/psum | solution.py:98
  111.1 52.6 %copy-start.13 = (f32[1,3072]{1,0:T(1,128)S(1)}, f32[1,3072]{1,0:T(1,128)}, u32[]{:S(2)}) copy-start(f32[1,3072]{1,0:T(1,128)} %get-tuple-element.27) | copy-start | bytes 36868
  111.1 129.4 %all-reduce.9.cloned.1.call-start = ((), (), s32[]{:S(2)}) async-start(), calls=%async_computation.2 | async-start | bytes 3145728 | tf_op jit(solution)/shard_map/psum | solution.py:96
  161.5 6.8 %slice-start = ((s8[4718592]{0:T(1024)(128)(4,1)}), s8[524288]{0:T(1024)(128)(4,1)S(1)}, s32[]{:S(2)}) async-start(s8[4718592]{0:T(1024)(128)(4,1)} %bitcast.184), calls=%async_computation.4 | async-start | bytes 1048576
  163.7 4.5 %slice-start.1 = ((s8[4718592]{0:T(1024)(128)(4,1)}), s8[4194304]{0:T(1024)(128)(4,1)S(1)}, s32[]{:S(2)}) async-start(s8[4718592]{0:T(1024)(128)(4,1)} %bitcast.184), calls=%async_computation.5 | async-start | bytes 8388608
  168.2 1.1 copy-start.15
  169.6 0.6 copy-start.5
  169.7 0.6 copy-start.7
  186.2 4.4 %copy-start.2 = (bf16[256,1,64]{0,2,1:T(8,128)(2,1)S(1)}, bf16[256,1,64]{0,2,1:T(8,128)(2,1)}, u32[]{:S(2)}) copy-start(bf16[256,1,64]{0,2,1:T(8,128)(2,1)} %copy-done.1) | copy-start | bytes 98308
  186.2 4.4 %copy-start.4 = (bf16[256,1,64]{0,2,1:T(8,128)(2,1)S(1)}, bf16[256,1,64]{0,2,1:T(8,128)(2,1)}, u32[]{:S(2)}) copy-start(bf16[256,1,64]{0,2,1:T(8,128)(2,1)} %copy-done.3) | copy-start | bytes 98308
  186.2 4.4 %copy-start.6 = (bf16[256,1,64]{0,2,1:T(8,128)(2,1)S(1)}, bf16[256,1,64]{0,2,1:T(8,128)(2,1)}, u32[]{:S(2)}) copy-start(bf16[256,1,64]{0,2,1:T(8,128)(2,1)} %copy-done.5) | copy-start | bytes 98308
  186.2 4.4 %copy-start.8 = (bf16[256,1,64]{0,2,1:T(8,128)(2,1)S(1)}, bf16[256,1,64]{0,2,1:T(8,128)(2,1)}, u32[]{:S(2)}) copy-start(bf16[256,1,64]{0,2,1:T(8,128)(2,1)} %copy-done.7) | copy-start | bytes 98308
  186.4 4.4 %copy-start.10 = (bf16[256,128]{1,0:T(8,128)(2,1)S(1)}, bf16[256,128]{1,0:T(8,128)(2,1)}, u32[]{:S(2)}) copy-start(bf16[256,128]{1,0:T(8,128)(2,1)} %get-tuple-element.36) | copy-start | bytes 196612
  186.4 4.4 %copy-start.11 = (bf16[256,128]{1,0:T(8,128)(2,1)S(1)}, bf16[256,128]{1,0:T(8,128)(2,1)}, u32[]{:S(2)}) copy-start(bf16[256,128]{1,0:T(8,128)(2,1)} %get-tuple-element.40) | copy-start | bytes 196612
  190.3 116.9 %all-reduce.11.cloned.1.call-start = ((), (), s32[]{:S(2)}) async-start(), calls=%async_computation.3 | async-start | bytes 3145728 | tf_op jit(solution)/shard_map/psum | solution.py:98
  247.3 9.6 %copy-start.9 = (pred[256,128]{1,0:T(8,128)(4,1)S(1)}, pred[256,128]{1,0:T(8,128)(4,1)}, u32[]{:S(2)}) copy-start(pred[256,128]{1,0:T(8,128)(4,1)} %get-tuple-element.33) | copy-start | bytes 98308
Sparse Core Ops, SparseCore 0:
  41.2 53.7 all-reduce.4
  111.3 50.1 all-reduce.6
  190.4 50.0 all-reduce.8
  257.0 50.1 all-reduce.10
where the time goes:
time: 317 us
  waiting for transfers between devices  181 us (57%)
  matrix products  74.3 us (23%)
  other arithmetic  42.6 us (13%)
  between operations  14.3 us (5%)
  local copies, waits for them, and re-layouts  3.94 us (1%)
    psum x4, waiting for transfers between devices, local_step(): hidden = hidden + lax.psum(part_out, 'tp')  181 us
    select_n x1, other arithmetic, write_rows(): return jnp.where(at_pos, rows[:, :, None], cache)  23 us
    dot_general x2, matrix products, mlp_block(): jnp.dot(activated, wd_layer, preferred_element_type=jnp.float32)  18.9 us
    dot_general x2, matrix products, attend_split(): jnp.einsum('bkgd,bskd->bkgs', query, k_old, preferred_element_type=jnp.fl...  15.9 us
    dot_general x2, matrix products, attend_split(): jnp.einsum('bkgs,bskd->bkgd', prob_old, v_old, preferred_element_type=jnp...  9.54 us
    dot_general x2, matrix products, mlp_block(): jnp.dot(normed, wg_layer, preferred_element_type=jnp.float32)  9.24 us
    reduce_sum x4, other arithmetic, rms_norm(): mean_sq = jnp.mean(hidden_f32 * hidden_f32, axis=-1, keepdims=True)  8.4 us
    dot_general x2, matrix products, attention_block(): jnp.dot(attended.reshape(batch_size, q_heads * head_dim), wo_layer, prefe...  7.67 us
  transfers between devices with their start and end apart: 4, of which 4 were waited for; matrix products, arithmetic and copies ran while one was open for 7% of the time, Pallas kernels for 0%

commit v1 on v0

v1 whole, which is shorter than its diff:
```python
import functools
import math

import jax
import jax.numpy as jnp
from jax import lax
from jax.experimental import pallas as pl
from jax.experimental.pallas import tpu as pltpu
from jax.sharding import PartitionSpec as P

F32 = jnp.float32
BF16 = jnp.bfloat16
MESH = pl.DeviceIdType.MESH
VMEM_BYTES = 64 * 1024 * 1024 - 128 * 1024
EPS = 1e-5


def rope_tables(positions, head_dim):
    half_dim = head_dim // 2
    inv_freq = jnp.power(500000.0, -jnp.arange(half_dim, dtype=jnp.float32) * (2.0 / head_dim))
    wavelen = (2.0 * math.pi) / inv_freq
    smooth = (8192.0 / wavelen - 1.0) / 3.0
    blended = (1.0 - smooth) * inv_freq / 8.0 + smooth * inv_freq
    scaled = jnp.where(wavelen < 2048.0, inv_freq, jnp.where(wavelen > 8192.0, inv_freq / 8.0, blended))
    angles = positions.astype(jnp.float32)[:, None] * scaled[None, :]
    return jnp.cos(angles), jnp.sin(angles)


def normed(x, gain):
    xf = x.astype(F32)
    mean_sq = jnp.mean(xf * xf, axis=-1, keepdims=True)
    return (xf * lax.rsqrt(mean_sq + EPS) * gain).astype(BF16)


def first_qkv_kernel(x_ref, g_ref, wq_ref, wk_ref, wv_ref, o_ref, h_ref):
    rows = x_ref.shape[0]
    qd = wq_ref.shape[2]
    kd = wk_ref.shape[2]
    gain = g_ref[0:1, :].astype(F32)

    @pl.loop(0, rows // 16)
    def _(i):
        sl = pl.ds(pl.multiple_of(i * 16, 16), 16)
        h_ref[sl, :] = normed(x_ref[sl, :], gain)

    h = h_ref[...]
    o_ref[:, 0:qd] = jnp.dot(h, wq_ref[0], preferred_element_type=F32).astype(BF16)
    o_ref[:, qd:qd + kd] = jnp.dot(h, wk_ref[0], preferred_element_type=F32).astype(BF16)
    o_ref[:, qd + kd:] = jnp.dot(h, wv_ref[0], preferred_element_type=F32).astype(BF16)


def first_qkv(hidden, attn_norm, w_query, w_key, w_value):
    rows, d = hidden.shape
    qd, kd = w_query.shape[2], w_key.shape[2]

    def first(shape):
        return pl.BlockSpec((1,) + shape, lambda i: (0, 0, 0))

    return pl.pallas_call(
        first_qkv_kernel,
        grid=(1,),
        in_specs=[
            pl.BlockSpec((rows, d), lambda i: (0, 0)),
            pl.BlockSpec(attn_norm.shape, lambda i: (0, 0)),
            first((d, qd)), first((d, kd)), first((d, kd)),
        ],
        out_specs=pl.BlockSpec((rows, qd + 2 * kd), lambda i: (0, 0)),
        out_shape=jax.ShapeDtypeStruct((rows, qd + 2 * kd), BF16),
        scratch_shapes=[pltpu.VMEM((rows, d), BF16)],
        compiler_params=pltpu.CompilerParams(vmem_limit_bytes=40 * 1024 * 1024),
        name="first_qkv",
    )(hidden, attn_norm, w_query, w_key, w_value)


BLOCK = 32


def attention_kernel(layer, pos_s, qkv_ref, cos_ref, sin_ref, posr_ref, k_ref, v_ref, *rest):
    o_ref, ko_ref, vo_ref = rest[-3:]
    step = pl.program_id(0)
    head = k_ref.shape[3]
    seq = k_ref.shape[2]
    heads = o_ref.shape[1] // head
    scale = head ** -0.5
    cos = cos_ref[...]
    sin = sin_ref[...]

    def rope(vec):
        return vec * cos + pltpu.roll(vec, head // 2, 1) * sin

    qs = [rope(qkv_ref[:, h * head:(h + 1) * head].astype(F32)) for h in range(heads)]
    kn = rope(qkv_ref[:, heads * head:(heads + 1) * head].astype(F32))
    vn = qkv_ref[:, (heads + 1) * head:(heads + 2) * head].astype(F32)

    seq_ids = lax.broadcasted_iota(jnp.int32, (seq // 16, 16, head), 0) * 16 + lax.broadcasted_iota(jnp.int32, (seq // 16, 16, head), 1)
    seq_bf = seq_ids.astype(F32).astype(BF16)
    row_of = lax.broadcasted_iota(jnp.int32, (32, head), 0) % 8
    lane = lax.broadcasted_iota(jnp.int32, (32, seq), 1)
    outs = []
    for j in range(BLOCK // 8):
        pieces = [q[8 * j:8 * j + 8] for q in qs]
        pieces += [jnp.zeros((8, head), F32)] * (4 - heads)
        qj = jnp.concatenate(pieces, axis=0).astype(BF16)
        scores = None
        for b8 in range(8):
            b = 8 * j + b8
            pos_b = pos_s[step * BLOCK + b].astype(F32)
            here = seq_bf == jnp.full((16, head), pos_b, F32).astype(BF16)[None]
            k_row = jnp.broadcast_to(kn[b:b + 1], (16, head)).astype(BF16)[None]
            v_row = jnp.broadcast_to(vn[b:b + 1], (16, head)).astype(BF16)[None]
            k_b = jnp.where(here, k_row, k_ref[0, b].reshape(seq // 16, 16, head)).reshape(seq, head)
            ko_ref[0, b] = k_b
            vo_ref[0, b] = jnp.where(here, v_row, v_ref[0, b].reshape(seq // 16, 16, head)).reshape(seq, head)
            s_b = lax.dot_general(qj, k_b, (((1,), (1,)), ((), ())), preferred_element_type=F32)
            scores = s_b if scores is None else jnp.where(row_of == b8, s_b, scores)
        scores = jnp.where(lane <= posr_ref[32 * j:32 * j + 32, :], scores * scale, -jnp.inf)
        peak = jnp.max(scores, axis=1, keepdims=True)
        weight = jnp.exp(scores - peak)
        total = jnp.sum(weight, axis=1, keepdims=True)
        prob = (weight * (1.0 / total)).astype(BF16)
        mixed = None
        for b8 in range(8):
            o_b = jnp.dot(prob, vo_ref[0, 8 * j + b8], preferred_element_type=F32)
            mixed = o_b if mixed is None else jnp.where(row_of == b8, o_b, mixed)
        outs.append(mixed)
    for h in range(heads):
        o_h = jnp.concatenate([m[8 * h:8 * h + 8] for m in outs], axis=0)
        o_ref[:, h * head:(h + 1) * head] = o_h.astype(BF16)


def attention(layer, qkv, cos2, sin2, posr, positions, k_cache, v_cache, k_prev, v_prev):
    layers, batch, seq, head = k_cache.shape
    qd = qkv.shape[1] - 2 * head
    cache_spec = pl.BlockSpec((1, BLOCK, seq, head), lambda i, p: (layer, i, 0, 0))
    row_spec = lambda width: pl.BlockSpec((BLOCK, width), lambda i, p: (i, 0))
    in_specs = [
        row_spec(qkv.shape[1]), row_spec(head), row_spec(head),
        pl.BlockSpec((BLOCK * 4, 1), lambda i, p: (i, 0)),
        cache_spec, cache_spec,
    ]
    args = [qkv, cos2, sin2, posr, k_cache, v_cache]
    aliases = {}
    if k_prev is not None:
        in_specs += [pl.BlockSpec(memory_space=pl.ANY)] * 2
        args += [k_prev, v_prev]
        aliases = {7: 1, 8: 2}
    return pl.pallas_call(
        functools.partial(attention_kernel, layer),
        grid_spec=pltpu.PrefetchScalarGridSpec(
            num_scalar_prefetch=1,
            grid=(batch // BLOCK,),
            in_specs=in_specs,
            out_specs=[row_spec(qd), cache_spec, cache_spec],
        ),
        out_shape=[
            jax.ShapeDtypeStruct((batch, qd), BF16),
            jax.ShapeDtypeStruct(k_cache.shape, BF16),
            jax.ShapeDtypeStruct(v_cache.shape, BF16),
        ],
        input_output_aliases=aliases,
        compiler_params=pltpu.CompilerParams(vmem_limit_bytes=40 * 1024 * 1024),
        name=f"attention_{layer}",
    )(positions, *args)


CHUNKS = 2


def mlp_kernel(layer, last, *refs):
    refs = list(refs)
    o_ref, x_hbm, gm_ref, ga_ref, wo_hbm, wg_hbm, wu_hbm, wd_hbm = refs[:8]
    refs = refs[8:]
    if last:
        x_out = refs[0]
        refs = refs[1:]
    else:
        wq_hbm, wk_hbm, wv_hbm, qkv_out, xres_out = refs[:5]
        refs = refs[5:]
    (wo, wg, wu, wd, xres, part, hbuf, abuf, d2d_in, rs_out, rs_in, acc, w_sem, x_sem,
     d2d_s, d2d_r, rs_s, rs_r, ag_s, ag_r, fw_s, fw_r) = refs[:22]
    refs = refs[22:]
    if last:
        (out_sem,) = refs
    else:
        wq, wk, wv = refs

    chunks, _, chips_n, own, d = part.shape
    rows = 8 * own
    ff = wg.shape[1]
    me = lax.axis_index("tp")
    group = lax.axis_index("dp")
    core = me % 2
    chip = me // 2
    chips = [chip, chip + 1 - 2 * (chip % 2), (chip + 2) % 4, 3 - chip]
    partner = (group, chip * 2 + 1 - core)
    peers = [None] + [(group, chips[k] * 2 + core) for k in (1, 2, 3)]
    order = (3, 1, 2)

    loads = [(wo_hbm, wo), (wg_hbm, wg), (wu_hbm, wu), (wd_hbm, wd)]
    nxt = layer
    if not last:
        loads += [(wq_hbm, wq), (wk_hbm, wk), (wv_hbm, wv)]
    load = []
    for i, (src, dst) in enumerate(loads):
        which = layer if i < 4 else layer + 1
        cp = pltpu.make_async_copy(src.at[which], dst, w_sem.at[i])
        cp.start()
        load.append(cp)
    x_loads = []
    for hh in range(chunks):
        src = x_hbm.at[hh, core, chip] if layer == 0 else x_hbm.at[hh]
        cp = pltpu.make_async_copy(src, xres.at[hh], x_sem.at[hh])
        cp.start()
        x_loads.append(cp)

    barrier = pltpu.get_barrier_semaphore()
    for dev in [partner] + peers[1:]:
        pl.semaphore_signal(barrier, inc=1, device_id=dev, device_id_type=MESH)
    pl.semaphore_wait(barrier, 4)

    def remote(src, dst, s, r, dev):
        return pltpu.make_async_remote_copy(
            src_ref=src, dst_ref=dst, send_sem=s, recv_sem=r, device_id=dev, device_id_type=MESH)

    def d2d(hh):
        return remote(part.at[hh, 1 - core], d2d_in.at[hh], d2d_s.at[hh], d2d_r.at[hh], partner)

    def rs(hh, k):
        return remote(rs_out.at[hh, k - 1], rs_in.at[hh, k - 1], rs_s.at[hh, k - 1], rs_r.at[hh, k - 1], peers[k])

    def ag(hh, k):
        ref = hbuf.at[hh, core, chip]
        return remote(ref, ref, ag_s.at[hh, k - 1], ag_r.at[hh, k - 1], peers[k])

    def ag_in(hh, k):
        ref = hbuf.at[hh, core, chips[k]]
        return remote(ref, ref, ag_s.at[hh, k - 1], ag_r.at[hh, k - 1], peers[k])

    def fw(hh, k):
        ref = hbuf.at[hh, core, chips[k]]
        return remote(ref, ref, fw_s.at[hh, k], fw_r.at[hh, k], partner)

    def fw_in(hh, k):
        ref = hbuf.at[hh, 1 - core, chips[k]]
        return remote(ref, ref, fw_s.at[hh, k], fw_r.at[hh, k], partner)

    def put_part(hh, cols, value):
        value = value.astype(BF16)
        for p in range(2):
            for c in range(4):
                at = (p * 4 + c) * own
                part[hh, p, c, :, cols] = value[at:at + own]

    def ph0(hh):
        d2d(hh).start()

    def ph1(hh):
        d2d(hh).wait_recv()
        for k in order:
            pair = part[hh, core, chips[k]].astype(F32) + d2d_in[hh, chips[k]].astype(F32)
            rs_out[hh, k - 1] = pair.astype(BF16)
            rs(hh, k).start()
        acc[hh] = part[hh, core, chip].astype(F32) + d2d_in[hh, chip].astype(F32)
        d2d(hh).wait_send()

    def ph2(hh, mode):
        for k in (1, 2, 3):
            rs(hh, k).wait_recv()
        total = acc[hh]
        for k in (1, 2, 3):
            total = total + rs_in[hh, k - 1].astype(F32)
        x = (xres[hh].astype(F32) + total.astype(BF16).astype(F32)).astype(BF16)
        if mode == "final":
            hbuf[hh, core, chip] = x
        else:
            xres[hh] = x
            gain = (gm_ref[layer:layer + 1, :] if mode == "mlp" else ga_ref[layer + 1:layer + 2, :]).astype(F32)
            hbuf[hh, core, chip] = normed(x, gain)
            if mode == "attn":
                xres_out[hh] = x
        for k in order:
            ag(hh, k).start()
        fw(hh, 0).start()
        for k in (1, 2, 3):
            rs(hh, k).wait_send()

    def ph3(hh):
        for k in (1, 2, 3):
            ag_in(hh, k).wait_recv()
            fw(hh, k).start()

    def ph4(hh):
        for k in range(4):
            fw_in(hh, k).wait_recv()
        for k in (1, 2, 3):
            ag(hh, k).wait_send()
        for k in range(4):
            fw(hh, k).wait_send()

    def out_product(hh):
        o = o_ref[hh * rows:(hh + 1) * rows, :]

        @pl.loop(0, d // 1024)
        def _(n):
            cols = pl.ds(pl.multiple_of(n * 1024, 1024), 1024)
            put_part(hh, cols, jnp.dot(o, wo[:, cols], preferred_element_type=F32))

    def gate_up(hh):
        h = hbuf[hh].reshape(rows, d)

        @pl.loop(0, ff // 256)
        def _(n):
            cols = pl.ds(pl.multiple_of(n * 256, 256), 256)
            g = jnp.dot(h, wg[:, cols], preferred_element_type=F32).astype(BF16).astype(F32)
            u = jnp.dot(h, wu[:, cols], preferred_element_type=F32).astype(BF16).astype(F32)
            abuf[:, cols] = (g * jax.nn.sigmoid(g) * u).astype(BF16)

    def down(hh):
        @pl.loop(0, d // 1024)
        def _(n):
            cols = pl.ds(pl.multiple_of(n * 1024, 1024), 1024)
            put_part(hh, cols, jnp.dot(abuf[...], wd[:, cols], preferred_element_type=F32))

    def next_qkv(hh):
        h = hbuf[hh].reshape(rows, d)
        qd, kd = wq.shape[1], wk.shape[1]
        at = slice(hh * rows, (hh + 1) * rows)
        qkv_out[at, 0:qd] = jnp.dot(h, wq[...], preferred_element_type=F32).astype(BF16)
        qkv_out[at, qd:qd + kd] = jnp.dot(h, wk[...], preferred_element_type=F32).astype(BF16)
        qkv_out[at, qd + kd:] = jnp.dot(h, wv[...], preferred_element_type=F32).astype(BF16)

    end = "final" if last else "attn"
    load[0].wait()
    for hh in range(chunks):
        out_product(hh)
        ph0(hh)
    for cp in x_loads:
        cp.wait()
    ph1(0)
    ph1(1)
    ph2(0, "mlp")
    ph2(1, "mlp")
    ph3(0)
    ph4(0)
    load[1].wait()
    load[2].wait()
    gate_up(0)
    ph3(1)
    load[3].wait()
    down(0)
    ph0(0)
    ph4(1)
    gate_up(1)
    ph1(0)
    down(1)
    ph0(1)
    ph1(1)
    ph2(0, end)
    ph2(1, end)
    if last:
        def put(hh):
            return pltpu.make_async_copy(hbuf.at[hh], x_out.at[hh], out_sem.at[hh])
        ph3(0)
        ph4(0)
        put(0).start()
        ph3(1)
        ph4(1)
        put(1).start()
        put(0).wait()
        put(1).wait()
    else:
        ph3(0)
        ph4(0)
        for i in (4, 5, 6):
            load[i].wait()
        next_qkv(0)
        ph3(1)
        ph4(1)
        next_qkv(1)


def sums_and_mlp(layer, last, o, x, mlp_norm, attn_norm, w_out, w_gate, w_up, w_down, w_query, w_key, w_value):
    batch, qd = o.shape
    d = w_out.shape[2]
    ff = w_gate.shape[2]
    kd = w_key.shape[2]
    own = batch // (8 * CHUNKS)
    rows = 8 * own
    vmem = pl.BlockSpec(memory_space=pltpu.VMEM)
    hbm = pl.BlockSpec(memory_space=pl.ANY)
    args = [o, x, mlp_norm, attn_norm, w_out, w_gate, w_up, w_down]
    in_specs = [vmem, hbm, vmem, vmem] + [hbm] * 4
    if last:
        out_shape = jax.ShapeDtypeStruct((CHUNKS, 2, 4, own, d), BF16)
        out_specs = hbm
    else:
        args += [w_query, w_key, w_value]
        in_specs += [hbm] * 3
        out_shape = [jax.ShapeDtypeStruct((batch, qd + 2 * kd), BF16), jax.ShapeDtypeStruct((CHUNKS, own, d), BF16)]
        out_specs = [vmem, vmem]
    dma = pltpu.SemaphoreType.DMA
    scratch = [
        pltpu.VMEM((qd, d), BF16), pltpu.VMEM((d, ff), BF16), pltpu.VMEM((d, ff), BF16), pltpu.VMEM((ff, d), BF16),
        pltpu.VMEM((CHUNKS, own, d), BF16),
        pltpu.VMEM((CHUNKS, 2, 4, own, d), BF16),
        pltpu.VMEM((CHUNKS, 2, 4, own, d), BF16),
        pltpu.VMEM((rows, ff), BF16),
        pltpu.VMEM((CHUNKS, 4, own, d), BF16),
        pltpu.VMEM((CHUNKS, 3, own, d), BF16),
        pltpu.VMEM((CHUNKS, 3, own, d), BF16),
        pltpu.VMEM((CHUNKS, own, d), F32),
        dma((7,)), dma((CHUNKS,)),
        dma((CHUNKS,)), dma((CHUNKS,)),
        dma((CHUNKS, 3)), dma((CHUNKS, 3)),
        dma((CHUNKS, 3)), dma((CHUNKS, 3)),
        dma((CHUNKS, 4)), dma((CHUNKS, 4)),
    ]
    if last:
        scratch += [dma((CHUNKS,))]
    else:
        scratch += [pltpu.VMEM((d, qd), BF16), pltpu.VMEM((d, kd), BF16), pltpu.VMEM((d, kd), BF16)]
    return pl.pallas_call(
        functools.partial(mlp_kernel, layer, last),
        in_specs=in_specs,
        out_specs=out_specs,
        out_shape=out_shape,
        scratch_shapes=scratch,
        compiler_params=pltpu.CompilerParams(
            vmem_limit_bytes=56 * 1024 * 1024, collective_id=layer, has_side_effects=True),
        name=f"sums_and_mlp_{layer}",
    )(*args)


def solution(mesh):
    row_spec = P('dp', None)
    pos_spec = P('dp')
    cache_spec = P(None, 'dp', None, 'tp', None)
    norm_spec = P(None, None)
    col_spec = P(None, None, 'tp')
    split_rows = P(None, 'tp', None)

    def local_step(hidden, positions, k_cache, v_cache, attn_norm, w_query, w_key, w_value, w_out, mlp_norm, w_gate, w_up, w_down):
        layers, batch, seq, _, head = k_cache.shape
        d = hidden.shape[1]
        own = batch // (8 * CHUNKS)
        kc = k_cache.reshape(layers, batch, seq, head)
        vc = v_cache.reshape(layers, batch, seq, head)
        cos_tab, sin_tab = rope_tables(positions, head)
        cos2 = jnp.concatenate([cos_tab, cos_tab], axis=1)
        sin2 = jnp.concatenate([-sin_tab, sin_tab], axis=1)
        posr = jnp.broadcast_to(positions.reshape(batch // 8, 1, 8), (batch // 8, 4, 8)).reshape(batch * 4, 1)
        qkv = first_qkv(hidden, attn_norm, w_query, w_key, w_value)
        x = hidden.reshape(CHUNKS, 2, 4, own, d)
        k_out = v_out = None
        for layer in range(layers):
            o, k_out, v_out = attention(layer, qkv, cos2, sin2, posr, positions, kc, vc, k_out, v_out)
            last = layer == layers - 1
            res = sums_and_mlp(layer, last, o, x, mlp_norm, attn_norm, w_out, w_gate, w_up, w_down, w_query, w_key, w_value)
            if last:
                hidden_out = res.reshape(batch, d)
            else:
                qkv, x = res
        return hidden_out, k_out.reshape(k_cache.shape), v_out.reshape(v_cache.shape)

    return jax.shard_map(local_step, mesh=mesh, in_specs=(row_spec, pos_spec, cache_spec, cache_spec, norm_spec, col_spec, col_spec, col_spec, split_rows, norm_spec, col_spec, col_spec, split_rows), out_specs=(row_spec, cache_spec, cache_spec), check_vma=False)
```

time: 317 us -> 171 us (0.54)
  waiting for transfers between devices: 181 us -> 0 us
  Pallas kernels: 0 us -> 154 us
  matrix products: 74.3 us -> 0 us
  other arithmetic: 42.6 us -> 1.38 us
  between operations: 14.3 us -> 0.72 us
  local copies, waits for them, and re-layouts: 3.94 us -> 13.9 us
    psum x4 -> x0, waiting for transfers between devices: 181 us -> none  [local_step(): hidden = hidden + lax.psum(part_out, 'tp')]
    pallas_call x0 -> x5, Pallas kernels: none -> 154 us  [the longest x2 111 us: sums_and_mlp(): pl.pallas_call(functools.partial(mlp_kernel, layer, last), in_specs=in_sp...]
    dot_general x16 -> x0, matrix products: 74.3 us -> none  [the longest x2 18.9 us: mlp_block(): jnp.dot(activated, wd_layer, preferred_element_type=jnp.float32)]
    select_n x1 -> x0, other arithmetic: 23 us -> none  [write_rows(): return jnp.where(at_pos, rows[:, :, None], cache)]
    unnamed x42 -> x21, local copies, waits for them, and re-layouts: 1.76 us -> 12.9 us
    reduce_sum x6 -> x0, other arithmetic: 9.76 us -> none  [the longest x4 8.4 us: rms_norm(): mean_sq = jnp.mean(hidden_f32 * hidden_f32, axis=-1, keepdims=True)]
  transfers between devices with their start and end apart: 4 -> 0, of which waited for: 4 -> 0; matrix products, arithmetic and copies ran while one was open for 7% -> 0% of each run, Pallas kernels for 0% -> 0%
where the time goes in v1:
time: 171 us; the launch traced here: 170 us
  Pallas kernels  154 us (90%)
  local copies, waits for them, and re-layouts  13.9 us (8%)
    pallas_call x2, Pallas kernels, sums_and_mlp(): pl.pallas_call(functools.partial(mlp_kernel, layer, last), in_specs=in_sp...  111 us
    pallas_call x2, Pallas kernels, attention(): pl.pallas_call(functools.partial(attention_kernel, layer), grid_spec=pltp...  39.5 us
    unnamed x21, local copies, waits for them, and re-layouts  12.9 us
    pallas_call x1, Pallas kernels, first_qkv(): pl.pallas_call(first_qkv_kernel, grid=(1,), in_specs=[pl.BlockSpec((rows,...  3.96 us

profile of v1, /device:TPU:0, one launch (start us, length us, event | category | flops | bytes accessed | tf_op | source)
XLA Modules:
  0.0 170.4 jit_solution(7736581166461379967)
XLA Ops:
  0.7 0.7 convert_element_type.3
  1.3 0.8 broadcast_in_dim.4
  2.1 0.0 copy-start
  2.1 2.3 %copy-done = bf16[2,3072,384]{2,1,0:T(8,128)(2,1)S(1)} copy-done((bf16[2,3072,384]{2,1,0:T(8,128)(2,1)S(1)}, bf16[2,3072,384]{2,1,0:T(8,128)(2,1)}, u32[]{:S(2)}) %copy-start) | copy-done | bytes 4718616
  4.5 0.0 copy-start.1
  4.5 1.4 copy-done.1
  5.9 0.0 copy-start.2
  5.9 1.4 copy-done.2
  7.3 0.0 copy-start.3
  7.3 1.4 copy-done.3
  8.7 0.0 copy-start.7
  8.7 0.7 copy-done.7
  9.4 4.0 %first_qkv.1.qkv_ref = bf16[256,640]{1,0:T(8,128)(2,1)S(1)} custom-call(bf16[256,3072]{1,0:T(8,128)(2,1)S(1)} %copy-done.1, bf16[2,3072]{1,0:T(2,128)(2,1)S(1)} %copy-done.7, bf16[2,3072,384]{2,1,0:T(8,128)(2,1)S(1)} %copy-done, bf16[2,3072,128]{2,1,0:T(8,128)(2,1)S(1)} %copy-done.2, bf16[2,3072,128]{2,1,0:T(8,128)(2,1)S(1)} %copy-done.3), custom_call_target="tpu_custom_call" | custom-call | tf_op jit(solution)/shard_map/first_qkv/pallas_call | solution.py:59
  13.4 0.5 fusion
  13.9 0.1 pad_maximum_fusion
  14.1 0.2 reshape.59.posr_ref
  14.3 0.0 copy-start.8
  14.3 0.7 copy-done.8
  14.9 19.7 %attention_0.1 = (bf16[256,384]{1,0:T(8,128)(2,1)S(1)}, bf16[2,256,128,128]{3,2,1,0:T(8,128)(2,1)}, bf16[2,256,128,128]{3,2,1,0:T(8,128)(2,1)}) custom-call(s32[256]{0:T(256)S(1)} %copy-done.8, bf16[256,640]{1,0:T(8,128)(2,1)S(1)} %first_qkv.1.qkv_ref, f32[256,128]{1,0:T(8,128)S(1)} %get-tuple-element.28.cos_ref, f32[256,128]{1,0:T(8,128)S(1)} %get-tuple-element.29.sin_ref, ...), custom_call_target="tpu_custom_call" | custom-call | tf_op jit(solution)/shard_map/attention_0/pallas_call | solution.py:147
  34.7 0.0 copy-start.6
  34.7 0.7 copy-done.6
  35.4 0.0 copy-start.9
  35.4 57.6 %sums_and_mlp_0.1 = (bf16[256,640]{1,0:T(8,128)(2,1)}, bf16[2,16,3072]{2,1,0:T(8,128)(2,1)}) custom-call(bf16[256,384]{1,0:T(8,128)(2,1)} %copy-done.6, bf16[2,2,4,16,3072]{4,3,2,1,0:T(8,128)(2,1)} %bitcast.10, bf16[2,3072]{1,0:T(2,128)(2,1)} %refs_2_.3, bf16[2,3072]{1,0:T(2,128)(2,1)} %refs_3_.3, bf16[2,384,3072]{2,1,0:T(8,128)(2,1)} %refs_4_.3, ...), custom_call_target="tpu_custom_call" | custom-call | tf_op jit(solution)/shard_map/sums_and_mlp_0/pallas_call | solution.py:422
  93.0 0.0 copy-done.9
  93.0 0.0 copy-start.4
  93.0 1.0 copy-done.4
  94.0 19.7 %attention_1.1 = (bf16[256,384]{1,0:T(8,128)(2,1)S(1)}, bf16[2,256,128,128]{3,2,1,0:T(8,128)(2,1)}, bf16[2,256,128,128]{3,2,1,0:T(8,128)(2,1)}) custom-call(s32[256]{0:T(256)S(1)} %copy-done.9, bf16[256,640]{1,0:T(8,128)(2,1)S(1)} %copy-done.4, f32[256,128]{1,0:T(8,128)S(1)} %get-tuple-element.28.cos_ref, ...), custom_call_target="tpu_custom_call", output_to_operand_aliasing={{1}: (7, {}), {2}: (8, {})} | custom-call | tf_op jit(solution)/shard_map/attention_1/pallas_call | solution.py:147
  113.7 0.0 copy-start.5
  113.7 0.7 copy-done.5
  114.4 53.3 %sums_and_mlp_1.1 = bf16[2,2,4,16,3072]{4,3,2,1,0:T(8,128)(2,1)} custom-call(bf16[256,384]{1,0:T(8,128)(2,1)} %copy-done.5, bf16[2,16,3072]{2,1,0:T(8,128)(2,1)} %get-tuple-element.16.refs_1_, bf16[2,3072]{1,0:T(2,128)(2,1)} %refs_2_.3, bf16[2,3072]{1,0:T(2,128)(2,1)} %refs_3_.3, bf16[2,384,3072]{2,1,0:T(8,128)(2,1)} %refs_4_.3, ...), custom_call_target="tpu_custom_call" | custom-call | tf_op jit(solution)/shard_map/sums_and_mlp_1/pallas_call | solution.py:422
  167.7 2.7 %copy.27 = bf16[256,3072]{1,0:T(8,128)(2,1)} copy(bf16[256,3072]{1,0:T(8,128)(2,1)} %bitcast.17) | data formatting | bytes 3145728
  (2 shorter events, 0.0 us)
Async XLA Ops:
  2.1 2.3 %copy-start = (bf16[2,3072,384]{2,1,0:T(8,128)(2,1)S(1)}, bf16[2,3072,384]{2,1,0:T(8,128)(2,1)}, u32[]{:S(2)}) copy-start(bf16[2,3072,384]{2,1,0:T(8,128)(2,1)} %refs_8_.1) | copy-start | bytes 14155780
  4.5 1.4 copy-start.1
  5.9 1.4 copy-start.2
  7.3 1.4 copy-start.3
  8.7 0.7 copy-start.7
  14.3 0.7 copy-start.8
  34.7 0.7 copy-start.6
  35.4 57.6 %copy-start.9 = (s32[256]{0:T(256)S(1)}, s32[256]{0:T(256)}, u32[]{:S(2)}) copy-start(s32[256]{0:T(256)} %pos_s.3) | copy-start | bytes 3076
  93.0 1.0 copy-start.4
  113.7 0.7 copy-start.5

commit v2 on v1

--- a/solution.py
+++ b/solution.py
@@ -32,42 +32,44 @@
     return (xf * lax.rsqrt(mean_sq + EPS) * gain).astype(BF16)
 
 
-def first_qkv_kernel(x_ref, g_ref, wq_ref, wk_ref, wv_ref, o_ref, h_ref):
-    rows = x_ref.shape[0]
-    qd = wq_ref.shape[2]
-    kd = wk_ref.shape[2]
+def first_qkv_kernel(x_hbm, g_ref, wq_hbm, wk_hbm, wv_hbm, o_ref, h_ref, wq, wk, wv, sem):
+    rows = h_ref.shape[0]
+    qd = wq.shape[1]
+    kd = wk.shape[1]
+    copies = [pltpu.make_async_copy(src, dst, sem.at[i]) for i, (src, dst) in enumerate(
+        [(x_hbm, h_ref), (wq_hbm.at[0], wq), (wk_hbm.at[0], wk), (wv_hbm.at[0], wv)])]
+    for cp in copies:
+        cp.start()
     gain = g_ref[0:1, :].astype(F32)
+    copies[0].wait()
 
     @pl.loop(0, rows // 16)
     def _(i):
         sl = pl.ds(pl.multiple_of(i * 16, 16), 16)
-        h_ref[sl, :] = normed(x_ref[sl, :], gain)
+        h_ref[sl, :] = normed(h_ref[sl, :], gain)
 
     h = h_ref[...]
-    o_ref[:, 0:qd] = jnp.dot(h, wq_ref[0], preferred_element_type=F32).astype(BF16)
-    o_ref[:, qd:qd + kd] = jnp.dot(h, wk_ref[0], preferred_element_type=F32).astype(BF16)
-    o_ref[:, qd + kd:] = jnp.dot(h, wv_ref[0], preferred_element_type=F32).astype(BF16)
+    copies[1].wait()
+    o_ref[:, 0:qd] = jnp.dot(h, wq[...], preferred_element_type=F32).astype(BF16)
+    copies[2].wait()
+    o_ref[:, qd:qd + kd] = jnp.dot(h, wk[...], preferred_element_type=F32).astype(BF16)
+    copies[3].wait()
+    o_ref[:, qd + kd:] = jnp.dot(h, wv[...], preferred_element_type=F32).astype(BF16)
 
 
 def first_qkv(hidden, attn_norm, w_query, w_key, w_value):
     rows, d = hidden.shape
     qd, kd = w_query.shape[2], w_key.shape[2]
-
-    def first(shape):
-        return pl.BlockSpec((1,) + shape, lambda i: (0, 0, 0))
-
+    vmem = pl.BlockSpec(memory_space=pltpu.VMEM)
+    hbm = pl.BlockSpec(memory_space=pl.ANY)
     return pl.pallas_call(
         first_qkv_kernel,
-        grid=(1,),
-        in_specs=[
-            pl.BlockSpec((rows, d), lambda i: (0, 0)),
-            pl.BlockSpec(attn_norm.shape, lambda i: (0, 0)),
-            first((d, qd)), first((d, kd)), first((d, kd)),
-        ],
-        out_specs=pl.BlockSpec((rows, qd + 2 * kd), lambda i: (0, 0)),
+        in_specs=[hbm, vmem, hbm, hbm, hbm],
+        out_specs=vmem,
         out_shape=jax.ShapeDtypeStruct((rows, qd + 2 * kd), BF16),
-        scratch_shapes=[pltpu.VMEM((rows, d), BF16)],
-        compiler_params=pltpu.CompilerParams(vmem_limit_bytes=40 * 1024 * 1024),
+        scratch_shapes=[pltpu.VMEM((rows, d), BF16), pltpu.VMEM((d, qd), BF16), pltpu.VMEM((d, kd), BF16),
+                        pltpu.VMEM((d, kd), BF16), pltpu.SemaphoreType.DMA((4,))],
+        compiler_params=pltpu.CompilerParams(vmem_limit_bytes=VMEM_BYTES),
         name="first_qkv",
     )(hidden, attn_norm, w_query, w_key, w_value)
 
@@ -75,57 +77,82 @@
 BLOCK = 32
 
 
-def attention_kernel(layer, pos_s, qkv_ref, cos_ref, sin_ref, posr_ref, k_ref, v_ref, *rest):
-    o_ref, ko_ref, vo_ref = rest[-3:]
-    step = pl.program_id(0)
-    head = k_ref.shape[3]
-    seq = k_ref.shape[2]
-    heads = o_ref.shape[1] // head
+def attend_block(qkv, cos, sin, posr, pos_at, k_at, v_at, k_put, v_put):
+    head = cos.shape[1]
+    seq = k_at(0).shape[0]
+    heads = qkv.shape[1] // head - 2
     scale = head ** -0.5
-    cos = cos_ref[...]
-    sin = sin_ref[...]
 
     def rope(vec):
+        vec = vec.astype(F32)
         return vec * cos + pltpu.roll(vec, head // 2, 1) * sin
 
-    qs = [rope(qkv_ref[:, h * head:(h + 1) * head].astype(F32)) for h in range(heads)]
-    kn = rope(qkv_ref[:, heads * head:(heads + 1) * head].astype(F32))
-    vn = qkv_ref[:, (heads + 1) * head:(heads + 2) * head].astype(F32)
-
-    seq_ids = lax.broadcasted_iota(jnp.int32, (seq // 16, 16, head), 0) * 16 + lax.broadcasted_iota(jnp.int32, (seq // 16, 16, head), 1)
+    qs = [rope(qkv[:, h * head:(h + 1) * head]) for h in range(heads)]
+    kn = rope(qkv[:, heads * head:(heads + 1) * head])
+    vn = qkv[:, (heads + 1) * head:(heads + 2) * head].astype(F32)
+
+    tiles = (seq // 16, 16, head)
+    seq_ids = lax.broadcasted_iota(jnp.int32, tiles, 0) * 16 + lax.broadcasted_iota(jnp.int32, tiles, 1)
     seq_bf = seq_ids.astype(F32).astype(BF16)
     row_of = lax.broadcasted_iota(jnp.int32, (32, head), 0) % 8
     lane = lax.broadcasted_iota(jnp.int32, (32, seq), 1)
-    outs = []
+
+    def updated(cache, row, b):
+        here = seq_bf == jnp.full((16, head), pos_at(b).astype(F32), F32).astype(BF16)[None]
+        row = jnp.broadcast_to(row, (16, head)).astype(BF16)[None]
+        return jnp.where(here, row, cache.reshape(tiles)).reshape(seq, head)
+
+    all_scores = []
     for j in range(BLOCK // 8):
-        pieces = [q[8 * j:8 * j + 8] for q in qs]
-        pieces += [jnp.zeros((8, head), F32)] * (4 - heads)
+        pieces = [q[8 * j:8 * j + 8] for q in qs] + [jnp.zeros((8, head), F32)] * (4 - heads)
         qj = jnp.concatenate(pieces, axis=0).astype(BF16)
         scores = None
         for b8 in range(8):
             b = 8 * j + b8
-            pos_b = pos_s[step * BLOCK + b].astype(F32)
-            here = seq_bf == jnp.full((16, head), pos_b, F32).astype(BF16)[None]
-            k_row = jnp.broadcast_to(kn[b:b + 1], (16, head)).astype(BF16)[None]
-            v_row = jnp.broadcast_to(vn[b:b + 1], (16, head)).astype(BF16)[None]
-            k_b = jnp.where(here, k_row, k_ref[0, b].reshape(seq // 16, 16, head)).reshape(seq, head)
-            ko_ref[0, b] = k_b
-            vo_ref[0, b] = jnp.where(here, v_row, v_ref[0, b].reshape(seq // 16, 16, head)).reshape(seq, head)
+            k_b = updated(k_at(b), kn[b:b + 1], b)
+            if k_put is not None:
+                k_put(b, k_b)
             s_b = lax.dot_general(qj, k_b, (((1,), (1,)), ((), ())), preferred_element_type=F32)
             scores = s_b if scores is None else jnp.where(row_of == b8, s_b, scores)
-        scores = jnp.where(lane <= posr_ref[32 * j:32 * j + 32, :], scores * scale, -jnp.inf)
+        all_scores.append(scores)
+    probs = []
+    for j in range(BLOCK // 8):
+        scores = jnp.where(lane <= posr[32 * j:32 * j + 32, :], all_scores[j] * scale, -jnp.inf)
         peak = jnp.max(scores, axis=1, keepdims=True)
         weight = jnp.exp(scores - peak)
         total = jnp.sum(weight, axis=1, keepdims=True)
-        prob = (weight * (1.0 / total)).astype(BF16)
+        probs.append((weight * (1.0 / total)).astype(BF16))
+    outs = []
+    for j in range(BLOCK // 8):
         mixed = None
         for b8 in range(8):
-            o_b = jnp.dot(prob, vo_ref[0, 8 * j + b8], preferred_element_type=F32)
+            b = 8 * j + b8
+            v_b = updated(v_at(b), vn[b:b + 1], b)
+            if v_put is not None:
+                v_put(b, v_b)
+            o_b = jnp.dot(probs[j], v_b, preferred_element_type=F32)
             mixed = o_b if mixed is None else jnp.where(row_of == b8, o_b, mixed)
         outs.append(mixed)
-    for h in range(heads):
-        o_h = jnp.concatenate([m[8 * h:8 * h + 8] for m in outs], axis=0)
-        o_ref[:, h * head:(h + 1) * head] = o_h.astype(BF16)
+    o = [jnp.concatenate([m[8 * h:8 * h + 8] for m in outs], axis=0).astype(BF16) for h in range(heads)]
+    return o, kn, vn
+
+
+def attention_kernel(pos_s, qkv_ref, cos_ref, sin_ref, posr_ref, k_ref, v_ref, *rest):
+    o_ref, ko_ref, vo_ref = rest[-3:]
+    step = pl.program_id(0)
+    head = k_ref.shape[3]
+
+    def k_put(b, value):
+        ko_ref[0, b] = value
+
+    def v_put(b, value):
+        vo_ref[0, b] = value
+
+    o, _, _ = attend_block(
+        qkv_ref[...], cos_ref[...], sin_ref[...], posr_ref[...], lambda b: pos_s[step * BLOCK + b],
+        lambda b: k_ref[0, b], lambda b: v_ref[0, b], k_put, v_put)
+    for h, o_h in enumerate(o):
+        o_ref[:, h * head:(h + 1) * head] = o_h
 
 
 def attention(layer, qkv, cos2, sin2, posr, positions, k_cache, v_cache, k_prev, v_prev):
@@ -145,7 +172,7 @@
         args += [k_prev, v_prev]
         aliases = {7: 1, 8: 2}
     return pl.pallas_call(
-        functools.partial(attention_kernel, layer),
+        attention_kernel,
         grid_spec=pltpu.PrefetchScalarGridSpec(
             num_scalar_prefetch=1,
             grid=(batch // BLOCK,),
@@ -158,7 +185,7 @@
             jax.ShapeDtypeStruct(v_cache.shape, BF16),
         ],
         input_output_aliases=aliases,
-        compiler_params=pltpu.CompilerParams(vmem_limit_bytes=40 * 1024 * 1024),
+        compiler_params=pltpu.CompilerParams(vmem_limit_bytes=VMEM_BYTES),
         name=f"attention_{layer}",
     )(positions, *args)
 
@@ -426,7 +453,7 @@
         out_shape=out_shape,
         scratch_shapes=scratch,
         compiler_params=pltpu.CompilerParams(
-            vmem_limit_bytes=56 * 1024 * 1024, collective_id=layer, has_side_effects=True),
+            vmem_limit_bytes=VMEM_BYTES, collective_id=layer, has_side_effects=True),
         name=f"sums_and_mlp_{layer}",
     )(*args)
 

time: 171 us -> 163 us (0.953)
  local copies, waits for them, and re-layouts: 13.9 us -> 4.42 us
  other arithmetic: 1.38 us -> 3.85 us
    unnamed x21 -> x1, local copies, waits for them, and re-layouts: 12.9 us -> 2.65 us
where the time goes in v2:
time: 163 us
  Pallas kernels  154 us (94%)
  local copies, waits for them, and re-layouts  4.42 us (3%)
  other arithmetic  3.85 us (2%)
    pallas_call x2, Pallas kernels, sums_and_mlp(): pl.pallas_call(functools.partial(mlp_kernel, layer, last), in_specs=in_sp...  111 us
    pallas_call x2, Pallas kernels, attention(): pl.pallas_call(attention_kernel, grid_spec=pltpu.PrefetchScalarGridSpec(n...  35.5 us
    pallas_call x1, Pallas kernels, first_qkv(): pl.pallas_call(first_qkv_kernel, in_specs=[hbm, vmem, hbm, hbm, hbm], out...  7.22 us

profile of v2, /device:TPU:0, one launch (start us, length us, event | category | flops | bytes accessed | tf_op | source)
XLA Modules:
  0.0 162.5 jit_solution(17262820202218366517)
XLA Ops:
  0.6 0.5 compare_select_fusion.1
  1.2 1.2 convert_element_type.3
  2.4 0.8 broadcast_in_dim.4
  3.2 7.2 %first_qkv.1.qkv_ref = bf16[256,640]{1,0:T(8,128)(2,1)} custom-call(bf16[256,3072]{1,0:T(8,128)(2,1)} %x_hbm.1, bf16[2,3072]{1,0:T(2,128)(2,1)} %refs_3_.3, bf16[2,3072,384]{2,1,0:T(8,128)(2,1)} %refs_8_.1, bf16[2,3072,128]{2,1,0:T(8,128)(2,1)} %refs_9_.1, bf16[2,3072,128]{2,1,0:T(8,128)(2,1)} %refs_10_.1), custom_call_target="tpu_custom_call" | custom-call | tf_op jit(solution)/shard_map/first_qkv/pallas_call | solution.py:65
  10.4 1.2 fusion
  11.7 0.8 pad_maximum_fusion
  12.5 1.0 reshape.59.posr_ref
  13.5 17.6 %attention_0.1 = (bf16[256,384]{1,0:T(8,128)(2,1)}, bf16[2,256,128,128]{3,2,1,0:T(8,128)(2,1)}, bf16[2,256,128,128]{3,2,1,0:T(8,128)(2,1)}) custom-call(s32[256]{0:T(256)} %pos_s.3, bf16[256,640]{1,0:T(8,128)(2,1)} %first_qkv.1.qkv_ref, f32[256,128]{1,0:T(8,128)} %get-tuple-element.28.cos_ref, f32[256,128]{1,0:T(8,128)} %get-tuple-element.29.sin_ref, ...), custom_call_target="tpu_custom_call" | custom-call | tf_op jit(solution)/shard_map/attention_0/pallas_call | solution.py:174
  31.1 57.6 %sums_and_mlp_0.1 = (bf16[256,640]{1,0:T(8,128)(2,1)}, bf16[2,16,3072]{2,1,0:T(8,128)(2,1)}) custom-call(bf16[256,384]{1,0:T(8,128)(2,1)} %get-tuple-element.11.refs_0_, bf16[2,2,4,16,3072]{4,3,2,1,0:T(8,128)(2,1)} %bitcast.16, bf16[2,3072]{1,0:T(2,128)(2,1)} %refs_2_.3, bf16[2,3072]{1,0:T(2,128)(2,1)} %refs_3_.3, bf16[2,384,3072]{2,1,0:T(8,128)(2,1)} %refs_4_.3, ...), custom_call_target="tpu_custom_call" | custom-call | tf_op jit(solution)/shard_map/sums_and_mlp_0/pallas_call | solution.py:449
  88.8 17.8 %attention_1.1 = (bf16[256,384]{1,0:T(8,128)(2,1)}, bf16[2,256,128,128]{3,2,1,0:T(8,128)(2,1)}, bf16[2,256,128,128]{3,2,1,0:T(8,128)(2,1)}) custom-call(s32[256]{0:T(256)} %pos_s.3, bf16[256,640]{1,0:T(8,128)(2,1)} %get-tuple-element.12.qkv_ref, f32[256,128]{1,0:T(8,128)} %get-tuple-element.28.cos_ref, ...), custom_call_target="tpu_custom_call", output_to_operand_aliasing={{1}: (7, {}), {2}: (8, {})} | custom-call | tf_op jit(solution)/shard_map/attention_1/pallas_call | solution.py:174
  106.6 53.3 %sums_and_mlp_1.1 = bf16[2,2,4,16,3072]{4,3,2,1,0:T(8,128)(2,1)} custom-call(bf16[256,384]{1,0:T(8,128)(2,1)} %get-tuple-element.15.refs_0_, bf16[2,16,3072]{2,1,0:T(8,128)(2,1)} %get-tuple-element.16.refs_1_, bf16[2,3072]{1,0:T(2,128)(2,1)} %refs_2_.3, bf16[2,3072]{1,0:T(2,128)(2,1)} %refs_3_.3, bf16[2,384,3072]{2,1,0:T(8,128)(2,1)} %refs_4_.3, ...), custom_call_target="tpu_custom_call" | custom-call | tf_op jit(solution)/shard_map/sums_and_mlp_1/pallas_call | solution.py:449
  159.9 2.7 %copy.27 = bf16[256,3072]{1,0:T(8,128)(2,1)} copy(bf16[256,3072]{1,0:T(8,128)(2,1)} %bitcast.17) | data formatting | bytes 3145728
  (1 shorter events, 0.0 us)

commit v3 on v0

v3 whole, which is shorter than its diff:
```python
import functools
import math

import jax
import jax.numpy as jnp
import numpy as np
from jax import lax
from jax.experimental import pallas as pl
from jax.experimental.pallas import tpu as pltpu
from jax.sharding import PartitionSpec as P

F32 = jnp.float32
BF16 = jnp.bfloat16
MESH = pl.DeviceIdType.MESH
VMEM_BYTES = 64 * 1024 * 1024 - 128 * 1024
EPS = 1e-5


def rope_rows(head_dim):
    half_dim = head_dim // 2
    f32 = np.float32
    inv_freq = np.power(f32(500000.0), -np.arange(half_dim, dtype=f32) * f32(2.0 / head_dim))
    wavelen = f32(2.0 * math.pi) / inv_freq
    smooth = (f32(8192.0) / wavelen - f32(1.0)) / f32(3.0)
    blended = (f32(1.0) - smooth) * inv_freq / f32(8.0) + smooth * inv_freq
    scaled = np.where(wavelen < 2048.0, inv_freq, np.where(wavelen > 8192.0, inv_freq / f32(8.0), blended)).astype(f32)
    ones = np.ones(half_dim, f32)
    return np.stack([np.concatenate([scaled, scaled]), np.concatenate([-ones, ones])])


def normed(x, gain):
    xf = x.astype(F32)
    mean_sq = jnp.mean(xf * xf, axis=-1, keepdims=True)
    return (xf * lax.rsqrt(mean_sq + EPS) * gain).astype(BF16)


BLOCK = 32


def attend_block(qkv, cos, sin, posc, pos_at, k_at, v_at, k_put, v_put):
    head = cos.shape[1]
    seq = k_at(0).shape[0]
    heads = qkv.shape[1] // head - 2
    scale = head ** -0.5

    def rope(vec):
        vec = vec.astype(F32)
        return vec * cos + pltpu.roll(vec, head // 2, 1) * sin

    qs = [rope(qkv[:, h * head:(h + 1) * head]) for h in range(heads)]
    kn = rope(qkv[:, heads * head:(heads + 1) * head])
    vn = qkv[:, (heads + 1) * head:(heads + 2) * head].astype(F32)

    tiles = (seq // 16, 16, head)
    seq_ids = lax.broadcasted_iota(jnp.int32, tiles, 0) * 16 + lax.broadcasted_iota(jnp.int32, tiles, 1)
    seq_bf = seq_ids.astype(F32).astype(BF16)
    row_of = lax.broadcasted_iota(jnp.int32, (32, head), 0) % 8
    lane = lax.broadcasted_iota(jnp.int32, (32, seq), 1).astype(F32)

    def updated(cache, row, b):
        here = seq_bf == jnp.full((16, head), pos_at(b).astype(F32), F32).astype(BF16)[None]
        row = jnp.broadcast_to(row, (16, head)).astype(BF16)[None]
        return jnp.where(here, row, cache.reshape(tiles)).reshape(seq, head)

    all_scores = []
    for j in range(BLOCK // 8):
        pieces = [q[8 * j:8 * j + 8] for q in qs] + [jnp.zeros((8, head), F32)] * (4 - heads)
        qj = jnp.concatenate(pieces, axis=0).astype(BF16)
        scores = None
        for b8 in range(8):
            b = 8 * j + b8
            k_b = updated(k_at(b), kn[b:b + 1], b)
            if k_put is not None:
                k_put(b, k_b)
            s_b = lax.dot_general(qj, k_b, (((1,), (1,)), ((), ())), preferred_element_type=F32)
            scores = s_b if scores is None else jnp.where(row_of == b8, s_b, scores)
        all_scores.append(scores)
    probs = []
    for j in range(BLOCK // 8):
        limit = jnp.concatenate([posc[8 * j:8 * j + 8]] * 4, axis=0)
        scores = jnp.where(lane <= limit, all_scores[j] * scale, -jnp.inf)
        peak = jnp.max(scores, axis=1, keepdims=True)
        weight = jnp.exp(scores - peak)
        total = jnp.sum(weight, axis=1, keepdims=True)
        probs.append((weight * (1.0 / total)).astype(BF16))
    outs = []
    for j in range(BLOCK // 8):
        mixed = None
        for b8 in range(8):
            b = 8 * j + b8
            v_b = updated(v_at(b), vn[b:b + 1], b)
            if v_put is not None:
                v_put(b, v_b)
            o_b = jnp.dot(probs[j], v_b, preferred_element_type=F32)
            mixed = o_b if mixed is None else jnp.where(row_of == b8, o_b, mixed)
        outs.append(mixed)
    o = [jnp.concatenate([m[8 * h:8 * h + 8] for m in outs], axis=0).astype(BF16) for h in range(heads)]
    return o, kn, vn


def first_kernel(
    pos_s, x_hbm, g_hbm, wq_hbm, wk_hbm, wv_hbm, pos_ref, rope_ref, k_hbm, v_hbm,
    o_ref, cos_ref, sin_ref, posc_ref, ko_hbm, vo_hbm,
    h_ref, g_ref, wq, wk, wv, qkv_ref, kbuf, vbuf, sem, in_sem, out_sem,
):
    rows = h_ref.shape[0]
    qd = wq.shape[1]
    kd = wk.shape[1]
    blocks = rows // BLOCK
    copies = [pltpu.make_async_copy(src, dst, sem.at[i]) for i, (src, dst) in enumerate(
        [(x_hbm, h_ref), (g_hbm, g_ref), (wq_hbm.at[0], wq), (wk_hbm.at[0], wk), (wv_hbm.at[0], wv)])]
    for cp in copies:
        cp.start()

    def reads(i):
        at = pl.ds(i * BLOCK, BLOCK)
        return (pltpu.make_async_copy(k_hbm.at[0, at], kbuf.at[at], in_sem.at[0, i]),
                pltpu.make_async_copy(v_hbm.at[0, at], vbuf.at[at], in_sem.at[1, i]))

    def writes(i):
        at = pl.ds(i * BLOCK, BLOCK)
        return (pltpu.make_async_copy(kbuf.at[at], ko_hbm.at[0, at], out_sem.at[0, i]),
                pltpu.make_async_copy(vbuf.at[at], vo_hbm.at[0, at], out_sem.at[1, i]))

    for i in range(blocks):
        for cp in reads(i):
            cp.start()

    width = pos_ref.shape[1]
    diagonal = (lax.broadcasted_iota(jnp.int32, (width, width), 0) == lax.broadcasted_iota(jnp.int32, (width, width), 1))
    for i in range(rows // width):
        across = jnp.broadcast_to(pos_ref[i:i + 1, :].astype(F32), (width, width))
        down = jnp.sum(jnp.where(diagonal, across, 0.0), axis=1, keepdims=True)
        at = slice(i * width, (i + 1) * width)
        angles = down * rope_ref[0:1, :]
        posc_ref[at, :] = jnp.broadcast_to(down, (width, width))
        cos_ref[at, :] = jnp.cos(angles)
        sin_ref[at, :] = jnp.sin(angles) * rope_ref[1:2, :]

    copies[0].wait()
    copies[1].wait()
    gain = g_ref[0:1, :].astype(F32)

    @pl.loop(0, rows // 16)
    def _(i):
        sl = pl.ds(pl.multiple_of(i * 16, 16), 16)
        h_ref[sl, :] = normed(h_ref[sl, :], gain)

    h = h_ref[...]
    copies[2].wait()
    qkv_ref[:, 0:qd] = jnp.dot(h, wq[...], preferred_element_type=F32).astype(BF16)
    copies[3].wait()
    copies[4].wait()
    qkv_ref[:, qd:qd + kd] = jnp.dot(h, wk[...], preferred_element_type=F32).astype(BF16)
    qkv_ref[:, qd + kd:] = jnp.dot(h, wv[...], preferred_element_type=F32).astype(BF16)

    @pl.loop(0, blocks)
    def _(i):
        base = pl.multiple_of(i * BLOCK, BLOCK)
        at = pl.ds(base, BLOCK)
        for cp in reads(i):
            cp.wait()

        def k_put(b, value):
            kbuf[base + b] = value

        def v_put(b, value):
            vbuf[base + b] = value

        o, _, _ = attend_block(
            qkv_ref[at, :], cos_ref[at, :], sin_ref[at, :], posc_ref[at, :], lambda b: pos_s[base + b],
            lambda b: kbuf[base + b], lambda b: vbuf[base + b], k_put, v_put)
        for n, o_n in enumerate(o):
            o_ref[at, n * kd:(n + 1) * kd] = o_n
        for cp in writes(i):
            cp.start()

    for i in range(blocks):
        for cp in writes(i):
            cp.wait()


def first(hidden, attn_norm, w_query, w_key, w_value, positions, k_cache, v_cache):
    rows, d = hidden.shape
    qd, kd = w_query.shape[2], w_key.shape[2]
    seq = k_cache.shape[2]
    blocks = rows // BLOCK
    vmem = pl.BlockSpec(memory_space=pltpu.VMEM)
    hbm = pl.BlockSpec(memory_space=pl.ANY)
    dma = pltpu.SemaphoreType.DMA
    table = jax.ShapeDtypeStruct((rows, kd), F32)
    cache = jax.ShapeDtypeStruct(k_cache.shape, BF16)
    return pl.pallas_call(
        first_kernel,
        in_specs=[pl.BlockSpec(memory_space=pltpu.SMEM)] + [hbm] * 5 + [vmem, vmem, hbm, hbm],
        out_specs=[vmem] * 4 + [hbm, hbm],
        out_shape=[jax.ShapeDtypeStruct((rows, qd), BF16), table, table, table, cache, cache],
        scratch_shapes=[
            pltpu.VMEM((rows, d), BF16), pltpu.VMEM(attn_norm.shape, BF16), pltpu.VMEM((d, qd), BF16),
            pltpu.VMEM((d, kd), BF16), pltpu.VMEM((d, kd), BF16), pltpu.VMEM((rows, qd + 2 * kd), BF16),
            pltpu.VMEM((rows, seq, kd), BF16), pltpu.VMEM((rows, seq, kd), BF16),
            dma((5,)), dma((2, blocks)), dma((2, blocks)),
        ],
        compiler_params=pltpu.CompilerParams(vmem_limit_bytes=VMEM_BYTES),
        name="first",
    )(positions, hidden, attn_norm, w_query, w_key, w_value, positions.reshape(rows // kd, kd),
      jnp.asarray(rope_rows(kd)), k_cache, v_cache)


def cache_kernel(layer, pos_s, kn_ref, vn_ref, k_hbm, v_hbm, k_prev, v_prev, ko_hbm, vo_hbm, kbuf, vbuf, in_sem, out_sem):
    batch, seq, head = kbuf.shape
    blocks = batch // BLOCK

    def reads(i):
        at = pl.ds(i * BLOCK, BLOCK)
        return (pltpu.make_async_copy(k_hbm.at[layer, at], kbuf.at[at], in_sem.at[0, i]),
                pltpu.make_async_copy(v_hbm.at[layer, at], vbuf.at[at], in_sem.at[1, i]))

    def writes(i):
        at = pl.ds(i * BLOCK, BLOCK)
        return (pltpu.make_async_copy(kbuf.at[at], ko_hbm.at[layer, at], out_sem.at[0, i]),
                pltpu.make_async_copy(vbuf.at[at], vo_hbm.at[layer, at], out_sem.at[1, i]))

    for i in range(blocks):
        for cp in reads(i):
            cp.start()
    row_of = lax.broadcasted_iota(jnp.int32, (16, head), 0)

    @pl.loop(0, blocks)
    def _(i):
        base = pl.multiple_of(i * BLOCK, BLOCK)
        at = pl.ds(base, BLOCK)
        new_rows = [(ref[at, :].astype(F32), buf) for ref, buf in ((kn_ref, kbuf), (vn_ref, vbuf))]
        for cp in reads(i):
            cp.wait()
        for b in range(BLOCK):
            pos = pos_s[base + b]
            tile = pl.ds(pl.multiple_of(pos // 16 * 16, 16), 16)
            here = row_of == pos % 16
            for rows, buf in new_rows:
                old = buf[base + b, tile, :].astype(F32)
                buf[base + b, tile, :] = jnp.where(here, rows[b:b + 1], old).astype(BF16)
        for cp in writes(i):
            cp.start()

    for i in range(blocks):
        for cp in writes(i):
            cp.wait()


def write_cache(layer, positions, k_rows, v_rows, k_cache, v_cache, k_prev, v_prev):
    layers, batch, seq, head = k_cache.shape
    blocks = batch // BLOCK
    vmem = pl.BlockSpec(memory_space=pltpu.VMEM)
    hbm = pl.BlockSpec(memory_space=pl.ANY)
    dma = pltpu.SemaphoreType.DMA
    return pl.pallas_call(
        functools.partial(cache_kernel, layer),
        in_specs=[pl.BlockSpec(memory_space=pltpu.SMEM), vmem, vmem] + [hbm] * 4,
        out_specs=[hbm, hbm],
        out_shape=[jax.ShapeDtypeStruct(k_cache.shape, BF16), jax.ShapeDtypeStruct(v_cache.shape, BF16)],
        input_output_aliases={5: 0, 6: 1},
        scratch_shapes=[pltpu.VMEM((batch, seq, head), BF16), pltpu.VMEM((batch, seq, head), BF16),
                        dma((2, blocks)), dma((2, blocks))],
        compiler_params=pltpu.CompilerParams(vmem_limit_bytes=VMEM_BYTES),
        name="write_cache",
    )(positions, k_rows, v_rows, k_cache, v_cache, k_prev, v_prev)


CHUNKS = 4

ORDER = (
    "O00O01O02O03P00P01P02S00P03S01S02F00",
    "G00D00F01S03P10G01F02D01G02P11F03D02",
    "S10G03P12D03S11P13F10Q20A20S12B20F11",
    "O20S13Q21P20A21F12B21O21Q22F13A22P21",
    "S20B22O22Q23A23P22B23S21O23F20P23G20",
    "D20S22F21P30G21D21S23F22P31G22S30D22",
    "F23P32G23S31D23F30P33S32E30F31E31S33",
    "F32E32F33E33",
)


def body_kernel(
    pos_s, o_hbm, x_hbm, gm_hbm, ga_hbm, wo_hbm, wg_hbm, wu_hbm, wd_hbm, wq_hbm, wk_hbm, wv_hbm, k_hbm, v_hbm,
    cos_hbm, sin_hbm, posc_hbm,
    x_out, kn_out, vn_out,
    wo, wg, wu, wd, wq, wk, wv, kbuf, vbuf, o_s, xres, part, hbuf, hst, abuf, qkv_s, d2d_in, rs_out, rs_in, acc,
    gm, ga, cos, sin, posc,
    w_sem, x_sem, kv_sem, t_sem, out_sem, d2d_s, d2d_r, rs_s, rs_r, ag_s, ag_r, fw_s, fw_r,
):
    chunks, _, _, own, d = part.shape
    rows = 8 * own
    ff = wg.shape[1]
    head = kbuf.shape[2]
    me = lax.axis_index("tp")
    group = lax.axis_index("dp")
    core = me % 2
    chip = me // 2
    chips = [chip, chip + 1 - 2 * (chip % 2), (chip + 2) % 4, 3 - chip]
    partner = (group, chip * 2 + 1 - core)
    peers = [None] + [(group, chips[k] * 2 + core) for k in (1, 2, 3)]
    order = (3, 1, 2)

    loads = {}

    def load(name, src, dst, sem):
        loads[name] = pltpu.make_async_copy(src, dst, sem)
        loads[name].start()

    def need(*names):
        for name in names:
            if name in loads:
                loads.pop(name).wait()

    load("o", o_hbm, o_s, t_sem.at[0])
    load("wo", wo_hbm.at[0], wo, w_sem.at[0])
    load("gm", gm_hbm, gm, t_sem.at[1])
    for q in range(chunks):
        load(("x", q), x_hbm.at[q, core, chip], xres.at[q], x_sem.at[q])
    load("wg", wg_hbm.at[0], wg, w_sem.at[1])
    load("wu", wu_hbm.at[0], wu, w_sem.at[2])
    load("wd", wd_hbm.at[0], wd, w_sem.at[3])
    load("ga", ga_hbm, ga, t_sem.at[2])
    load("wq", wq_hbm.at[1], wq, w_sem.at[4])
    load("wk", wk_hbm.at[1], wk, w_sem.at[5])
    load("wv", wv_hbm.at[1], wv, w_sem.at[6])
    load("cos", cos_hbm, cos, t_sem.at[3])
    load("sin", sin_hbm, sin, t_sem.at[4])
    load("posc", posc_hbm, posc, t_sem.at[5])

    def load_kv(i):
        at = pl.ds(i * BLOCK, BLOCK)
        load(("k", i), k_hbm.at[1, at], kbuf.at[at], kv_sem.at[0, i])
        load(("v", i), v_hbm.at[1, at], vbuf.at[at], kv_sem.at[1, i])

    barrier = pltpu.get_barrier_semaphore()
    for dev in [partner] + peers[1:]:
        pl.semaphore_signal(barrier, inc=1, device_id=dev, device_id_type=MESH)
    pl.semaphore_wait(barrier, 4)

    def remote(src, dst, s, r, dev):
        return pltpu.make_async_remote_copy(
            src_ref=src, dst_ref=dst, send_sem=s, recv_sem=r, device_id=dev, device_id_type=MESH)

    def d2d(q):
        return remote(part.at[q, 1 - core], d2d_in.at[q], d2d_s.at[q], d2d_r.at[q], partner)

    def rs(q, k):
        return remote(rs_out.at[q, k - 1], rs_in.at[q, k - 1], rs_s.at[q, k - 1], rs_r.at[q, k - 1], peers[k])

    def ag(q, k):
        ref = hbuf.at[q, core, chip]
        return remote(ref, ref, ag_s.at[q, k - 1], ag_r.at[q, k - 1], peers[k])

    def ag_in(q, k):
        ref = hbuf.at[q, core, chips[k]]
        return remote(ref, ref, ag_s.at[q, k - 1], ag_r.at[q, k - 1], peers[k])

    def fw(q, k):
        ref = hbuf.at[q, core, chips[k]]
        return remote(ref, ref, fw_s.at[q, k], fw_r.at[q, k], partner)

    def fw_in(q, k):
        ref = hbuf.at[q, 1 - core, chips[k]]
        return remote(ref, ref, fw_s.at[q, k], fw_r.at[q, k], partner)

    def put_part(q, cols, value):
        for p in range(2):
            for c in range(4):
                at = (p * 4 + c) * own
                part[q, p, c, :, cols] = value[at:at + own].astype(BF16)

    def pair_sums(q):
        d2d(q).wait_recv()
        for k in order:
            pair = part[q, core, chips[k]].astype(F32) + d2d_in[q, chips[k]].astype(F32)
            rs_out[q, k - 1] = pair.astype(BF16)
            rs(q, k).start()
        acc[q] = part[q, core, chip].astype(F32) + d2d_in[q, chip].astype(F32)
        d2d(q).wait_send()

    def totals(a, q):
        for k in (1, 2, 3):
            rs(q, k).wait_recv()
        need(("x", q))
        total = acc[q]
        for k in (1, 2, 3):
            total = total + rs_in[q, k - 1].astype(F32)
        x = (xres[q].astype(F32) + total.astype(BF16).astype(F32)).astype(BF16)
        if a == 3:
            hbuf[q, core, chip] = x
        else:
            xres[q] = x
            if a == 1:
                need("ga")
                gain = ga[1:2, :]
            else:
                need("gm")
                gain = gm[a // 2:a // 2 + 1, :]
            hbuf[q, core, chip] = normed(x, gain.astype(F32))
        for k in order:
            ag(q, k).start()
        fw(q, 0).start()
        for k in (1, 2, 3):
            rs(q, k).wait_send()

    def forward(q):
        for k in (1, 2, 3):
            ag_in(q, k).wait_recv()
            fw(q, k).start()

    def gathered(q):
        for k in range(4):
            fw_in(q, k).wait_recv()
        for k in (1, 2, 3):
            ag(q, k).wait_send()
        for k in range(4):
            fw(q, k).wait_send()

    def stage(q):
        gathered(q)
        hst[...] = hbuf[q].reshape(rows, d)

    def out_product(a, q):
        need("o", "wo")

        @pl.loop(0, d // 1024)
        def _(n):
            cols = pl.ds(pl.multiple_of(n * 1024, 1024), 1024)
            put_part(q, cols, jnp.dot(o_s[q * rows:(q + 1) * rows, :], wo[:, cols], preferred_element_type=F32))

        d2d(q).start()

    def gate_up(q):
        stage(q)
        need("wg", "wu")

        @pl.loop(0, ff // 256)
        def _(n):
            cols = pl.ds(pl.multiple_of(n * 256, 256), 256)
            h = hst[...]
            g = jnp.dot(h, wg[:, cols], preferred_element_type=F32).astype(BF16).astype(F32)
            u = jnp.dot(h, wu[:, cols], preferred_element_type=F32).astype(BF16).astype(F32)
            abuf[q, :, cols] = (g * jax.nn.sigmoid(g) * u).astype(BF16)

    def down(q):
        need("wd")

        @pl.loop(0, d // 1024)
        def _(n):
            cols = pl.ds(pl.multiple_of(n * 1024, 1024), 1024)
            put_part(q, cols, jnp.dot(abuf[q], wd[:, cols], preferred_element_type=F32))

        d2d(q).start()

    def qkv(q):
        stage(q)
        need("wq", "wk", "wv")
        qd, kd = wq.shape[1], wk.shape[1]
        h = hst[...]
        qkv_s[q, :, 0:qd] = jnp.dot(h, wq[...], preferred_element_type=F32).astype(BF16)
        qkv_s[q, :, qd:qd + kd] = jnp.dot(h, wk[...], preferred_element_type=F32).astype(BF16)
        qkv_s[q, :, qd + kd:] = jnp.dot(h, wv[...], preferred_element_type=F32).astype(BF16)

    def attend(q, i):
        need("cos", "sin", "posc")
        for j in range(rows // BLOCK // 2):
            first = i * (rows // 2) + j * BLOCK
            block = (q * rows + first) // BLOCK
            need(("k", block), ("v", block))
            base = block * BLOCK
            at = slice(base, base + BLOCK)
            o, kn, vn = attend_block(
                qkv_s[q, first:first + BLOCK, :], cos[at, :], sin[at, :], posc[at, :], lambda b: pos_s[base + b],
                lambda b: kbuf[base + b], lambda b: vbuf[base + b], None, None)
            for h, o_h in enumerate(o):
                o_s[at, h * head:(h + 1) * head] = o_h
            kn_out[at, :] = kn.astype(BF16)
            vn_out[at, :] = vn.astype(BF16)

    def result(q):
        gathered(q)
        load(("out", q), hbuf.at[q], x_out.at[q], out_sem.at[q])

    steps = [line[i:i + 3] for line in ORDER for i in range(0, len(line), 3)]
    last = {name: max(i for i, s in enumerate(steps) if s[0] == name and s[1] == "0") for name in "OGD"}
    for i, code in enumerate(steps):
        name, a, q = code[0], int(code[1]), int(code[2])
        if name == "O":
            out_product(a, q)
        elif name == "P":
            pair_sums(q)
        elif name == "S":
            totals(a, q)
        elif name == "F":
            forward(q)
        elif name == "G":
            gate_up(q)
        elif name == "D":
            down(q)
        elif name == "Q":
            qkv(q)
        elif name in "AB":
            attend(q, "AB".index(name))
        else:
            result(q)
        if i == last["O"]:
            load("wo", wo_hbm.at[1], wo, w_sem.at[0])
            for j in range(kbuf.shape[0] // BLOCK):
                load_kv(j)
        if i == last["G"]:
            load("wg", wg_hbm.at[1], wg, w_sem.at[1])
            load("wu", wu_hbm.at[1], wu, w_sem.at[2])
        if i == last["D"]:
            load("wd", wd_hbm.at[1], wd, w_sem.at[3])
    need(*[("out", q) for q in range(chunks)])


def body(positions, o, x, mlp_norm, attn_norm, w_out, w_gate, w_up, w_down, w_query, w_key, w_value, k_cache, v_cache, cos2, sin2, posc):
    batch, qd = o.shape
    d = w_out.shape[2]
    ff = w_gate.shape[2]
    kd = w_key.shape[2]
    seq = k_cache.shape[2]
    own = batch // (8 * CHUNKS)
    rows = 8 * own
    vmem = pl.BlockSpec(memory_space=pltpu.VMEM)
    hbm = pl.BlockSpec(memory_space=pl.ANY)
    dma = pltpu.SemaphoreType.DMA
    row = jax.ShapeDtypeStruct((batch, kd), BF16)
    return pl.pallas_call(
        body_kernel,
        in_specs=[pl.BlockSpec(memory_space=pltpu.SMEM)] + [hbm] * 16,
        out_specs=[hbm, vmem, vmem],
        out_shape=[jax.ShapeDtypeStruct((CHUNKS, 2, 4, own, d), BF16), row, row],
        scratch_shapes=[
            pltpu.VMEM((qd, d), BF16), pltpu.VMEM((d, ff), BF16), pltpu.VMEM((d, ff), BF16), pltpu.VMEM((ff, d), BF16),
            pltpu.VMEM((d, qd), BF16), pltpu.VMEM((d, kd), BF16), pltpu.VMEM((d, kd), BF16),
            pltpu.VMEM((batch, seq, kd), BF16), pltpu.VMEM((batch, seq, kd), BF16),
            pltpu.VMEM((batch, qd), BF16),
            pltpu.VMEM((CHUNKS, own, d), BF16),
            pltpu.VMEM((CHUNKS, 2, 4, own, d), BF16),
            pltpu.VMEM((CHUNKS, 2, 4, own, d), BF16),
            pltpu.VMEM((rows, d), BF16),
            pltpu.VMEM((CHUNKS, rows, ff), BF16),
            pltpu.VMEM((CHUNKS, rows, qd + 2 * kd), BF16),
            pltpu.VMEM((CHUNKS, 4, own, d), BF16),
            pltpu.VMEM((CHUNKS, 3, own, d), BF16),
            pltpu.VMEM((CHUNKS, 3, own, d), BF16),
            pltpu.VMEM((CHUNKS, own, d), F32),
            pltpu.VMEM(mlp_norm.shape, BF16), pltpu.VMEM(attn_norm.shape, BF16),
            pltpu.VMEM((batch, kd), F32), pltpu.VMEM((batch, kd), F32), pltpu.VMEM((batch, kd), F32),
            dma((7,)), dma((CHUNKS,)), dma((2, batch // BLOCK)), dma((6,)), dma((CHUNKS,)),
            dma((CHUNKS,)), dma((CHUNKS,)),
            dma((CHUNKS, 3)), dma((CHUNKS, 3)),
            dma((CHUNKS, 3)), dma((CHUNKS, 3)),
            dma((CHUNKS, 4)), dma((CHUNKS, 4)),
        ],
        compiler_params=pltpu.CompilerParams(vmem_limit_bytes=VMEM_BYTES, collective_id=0, has_side_effects=True),
        name="body",
    )(positions, o, x, mlp_norm, attn_norm, w_out, w_gate, w_up, w_down, w_query, w_key, w_value, k_cache, v_cache, cos2, sin2, posc)


def solution(mesh):
    row_spec = P('dp', None)
    pos_spec = P('dp')
    cache_spec = P(None, 'dp', None, 'tp', None)
    norm_spec = P(None, None)
    col_spec = P(None, None, 'tp')
    split_rows = P(None, 'tp', None)

    def local_step(hidden, positions, k_cache, v_cache, attn_norm, w_query, w_key, w_value, w_out, mlp_norm, w_gate, w_up, w_down):
        layers, batch, seq, _, head = k_cache.shape
        d = hidden.shape[1]
        own = batch // (8 * CHUNKS)
        kc = k_cache.reshape(layers, batch, seq, head)
        vc = v_cache.reshape(layers, batch, seq, head)
        o, cos2, sin2, posc, k_out, v_out = first(hidden, attn_norm, w_query, w_key, w_value, positions, kc, vc)
        x = hidden.reshape(CHUNKS, 2, 4, own, d)
        x_out, k_rows, v_rows = body(positions, o, x, mlp_norm, attn_norm, w_out, w_gate, w_up, w_down,
                                     w_query, w_key, w_value, kc, vc, cos2, sin2, posc)
        k_out, v_out = write_cache(1, positions, k_rows, v_rows, kc, vc, k_out, v_out)
        return x_out.reshape(batch, d), k_out.reshape(k_cache.shape), v_out.reshape(v_cache.shape)

    return jax.shard_map(local_step, mesh=mesh, in_specs=(row_spec, pos_spec, cache_spec, cache_spec, norm_spec, col_spec, col_spec, col_spec, split_rows, norm_spec, col_spec, col_spec, split_rows), out_specs=(row_spec, cache_spec, cache_spec), check_vma=False)
```

time: 317 us -> 134 us (0.42)
  waiting for transfers between devices: 181 us -> 0 us
  Pallas kernels: 0 us -> 130 us
  matrix products: 74.3 us -> 0 us
  other arithmetic: 42.6 us -> 0 us
  between operations: 14.3 us -> 0.65 us
    psum x4 -> x0, waiting for transfers between devices: 181 us -> none  [local_step(): hidden = hidden + lax.psum(part_out, 'tp')]
    pallas_call x0 -> x3, Pallas kernels: none -> 130 us  [the longest x1 96.7 us: body(): pl.pallas_call(body_kernel, in_specs=[pl.BlockSpec(memory_space=pltpu.SME...]
    dot_general x16 -> x0, matrix products: 74.3 us -> none  [the longest x2 18.9 us: mlp_block(): jnp.dot(activated, wd_layer, preferred_element_type=jnp.float32)]
    select_n x2 -> x0, other arithmetic: 23 us -> none  [the longest x1 23 us: write_rows(): return jnp.where(at_pos, rows[:, :, None], cache)]
    reduce_sum x6 -> x0, other arithmetic: 9.76 us -> none  [the longest x4 8.4 us: rms_norm(): mean_sq = jnp.mean(hidden_f32 * hidden_f32, axis=-1, keepdims=True)]
  transfers between devices with their start and end apart: 4 -> 0, of which waited for: 4 -> 0; matrix products, arithmetic and copies ran while one was open for 7% -> 0% of each run, Pallas kernels for 0% -> 0%
where the time goes in v3:
time: 134 us
  Pallas kernels  130 us (97%)
  local copies, waits for them, and re-layouts  2.65 us (2%)
    pallas_call x1, Pallas kernels, body(): pl.pallas_call(body_kernel, in_specs=[pl.BlockSpec(memory_space=pltpu.SME...  96.7 us
    pallas_call x1, Pallas kernels, first(): pl.pallas_call(first_kernel, in_specs=[pl.BlockSpec(memory_space=pltpu.SM...  20.7 us
    pallas_call x1, Pallas kernels, write_cache(): pl.pallas_call(functools.partial(cache_kernel, layer), in_specs=[pl.Block...  13 us

profile of v3, /device:TPU:0, one launch (start us, length us, event | category | flops | bytes accessed | tf_op | source)
XLA Modules:
  0.0 133.8 jit_solution(5996542670216245740)
XLA Ops:
  0.6 20.7 %first.1 = (bf16[256,384]{1,0:T(8,128)(2,1)}, f32[256,128]{1,0:T(8,128)}, f32[256,128]{1,0:T(8,128)}, f32[256,128]{1,0:T(8,128)}, bf16[2,256,128,128]{3,2,1,0:T(...) custom-call(s32[256]{0:T(256)} %pos_s.5, bf16[256,3072]{1,0:T(8,128)(2,1)} %x_hbm.1, bf16[2,3072]{1,0:T(2,128)(2,1)} %ga_hbm.1, ...), custom_call_target="tpu_custom_call" | custom-call | tf_op jit(solution)/shard_map/first/pallas_call | solution.py:193
  21.4 96.7 %body.1 = (bf16[4,2,4,8,3072]{4,3,2,1,0:T(8,128)(2,1)}, bf16[256,128]{1,0:T(8,128)(2,1)}, bf16[256,128]{1,0:T(8,128)(2,1)}) custom-call(s32[256]{0:T(256)} %pos_s.5, bf16[256,384]{1,0:T(8,128)(2,1)} %get-tuple-element.14.o_hbm, bf16[4,2,4,8,3072]{4,3,2,1,0:T(8,128)(2,1)} %bitcast.19, bf16[2,3072]{1,0:T(2,128)(2,1)} %gm_hbm.1, bf16[2,3072]{1,0:T(2,128)(2,1)} %ga_hbm.1, ...), custom_call_target="tpu_custom_call" | custom-call | tf_op jit(solution)/shard_map/body/pallas_call | solution.py:532
  118.1 13.0 %write_cache.1 = (bf16[2,256,128,128]{3,2,1,0:T(8,128)(2,1)}, bf16[2,256,128,128]{3,2,1,0:T(8,128)(2,1)}) custom-call(s32[256]{0:T(256)} %pos_s.5, bf16[256,128]{1,0:T(8,128)(2,1)} %get-tuple-element.19.kn_ref, bf16[256,128]{1,0:T(8,128)(2,1)} %get-tuple-element.20.vn_ref, ...), custom_call_target="tpu_custom_call", output_to_operand_aliasing={{0}: (5, {}), {1}: (6, {})} | custom-call | tf_op jit(solution)/shard_map/write_cache/pallas_call | solution.py:257
  131.1 2.7 %copy.24 = bf16[256,3072]{1,0:T(8,128)(2,1)} copy(bf16[256,3072]{1,0:T(8,128)(2,1)} %bitcast.20) | data formatting | bytes 3145728

commit v4 on v3

--- a/solution.py
+++ b/solution.py
@@ -122,10 +122,6 @@
         return (pltpu.make_async_copy(kbuf.at[at], ko_hbm.at[0, at], out_sem.at[0, i]),
                 pltpu.make_async_copy(vbuf.at[at], vo_hbm.at[0, at], out_sem.at[1, i]))
 
-    for i in range(blocks):
-        for cp in reads(i):
-            cp.start()
-
     width = pos_ref.shape[1]
     diagonal = (lax.broadcasted_iota(jnp.int32, (width, width), 0) == lax.broadcasted_iota(jnp.int32, (width, width), 1))
     for i in range(rows // width):
@@ -139,6 +135,9 @@
 
     copies[0].wait()
     copies[1].wait()
+    for i in range(blocks):
+        for cp in reads(i):
+            cp.start()
     gain = g_ref[0:1, :].astype(F32)
 
     @pl.loop(0, rows // 16)
@@ -207,9 +206,16 @@
       jnp.asarray(rope_rows(kd)), k_cache, v_cache)
 
 
-def cache_kernel(layer, pos_s, kn_ref, vn_ref, k_hbm, v_hbm, k_prev, v_prev, ko_hbm, vo_hbm, kbuf, vbuf, in_sem, out_sem):
+def cache_kernel(
+    layer, pos_s, kn_ref, vn_ref, x_hbm, k_hbm, v_hbm, k_prev, v_prev,
+    x_out, ko_hbm, vo_hbm,
+    kbuf, vbuf, xbuf, in_sem, out_sem, x_sem,
+):
     batch, seq, head = kbuf.shape
     blocks = batch // BLOCK
+    x_in = pltpu.make_async_copy(x_hbm, xbuf, x_sem.at[0])
+    x_in.start()
+    x_put = pltpu.make_async_copy(xbuf, x_out, x_sem.at[1])
 
     def reads(i):
         at = pl.ds(i * BLOCK, BLOCK)
@@ -243,12 +249,15 @@
         for cp in writes(i):
             cp.start()
 
+    x_in.wait()
+    x_put.start()
     for i in range(blocks):
         for cp in writes(i):
             cp.wait()
-
-
-def write_cache(layer, positions, k_rows, v_rows, k_cache, v_cache, k_prev, v_prev):
+    x_put.wait()
+
+
+def write_cache(layer, positions, k_rows, v_rows, x, k_cache, v_cache, k_prev, v_prev):
     layers, batch, seq, head = k_cache.shape
     blocks = batch // BLOCK
     vmem = pl.BlockSpec(memory_space=pltpu.VMEM)
@@ -256,28 +265,26 @@
     dma = pltpu.SemaphoreType.DMA
     return pl.pallas_call(
         functools.partial(cache_kernel, layer),
-        in_specs=[pl.BlockSpec(memory_space=pltpu.SMEM), vmem, vmem] + [hbm] * 4,
-        out_specs=[hbm, hbm],
-        out_shape=[jax.ShapeDtypeStruct(k_cache.shape, BF16), jax.ShapeDtypeStruct(v_cache.shape, BF16)],
-        input_output_aliases={5: 0, 6: 1},
-        scratch_shapes=[pltpu.VMEM((batch, seq, head), BF16), pltpu.VMEM((batch, seq, head), BF16),
-                        dma((2, blocks)), dma((2, blocks))],
+        in_specs=[pl.BlockSpec(memory_space=pltpu.SMEM), vmem, vmem] + [hbm] * 5,
+        out_specs=[hbm] * 3,
+        out_shape=[jax.ShapeDtypeStruct(a.shape, BF16) for a in (x, k_cache, v_cache)],
+        input_output_aliases={6: 1, 7: 2},
+        scratch_shapes=[pltpu.VMEM((batch, seq, head), BF16), pltpu.VMEM((batch, seq, head), BF16), pltpu.VMEM(x.shape, BF16),
+                        dma((2, blocks)), dma((2, blocks)), dma((2,))],
         compiler_params=pltpu.CompilerParams(vmem_limit_bytes=VMEM_BYTES),
         name="write_cache",
-    )(positions, k_rows, v_rows, k_cache, v_cache, k_prev, v_prev)
+    )(positions, k_rows, v_rows, x, k_cache, v_cache, k_prev, v_prev)
 
 
 CHUNKS = 4
 
 ORDER = (
-    "O00O01O02O03P00P01P02S00P03S01S02F00",
-    "G00D00F01S03P10G01F02D01G02P11F03D02",
-    "S10G03P12D03S11P13F10Q20A20S12B20F11",
-    "O20S13Q21P20A21F12B21O21Q22F13A22P21",
-    "S20B22O22Q23A23P22B23S21O23F20P23G20",
-    "D20S22F21P30G21D21S23F22P31G22S30D22",
-    "F23P32G23S31D23F30P33S32E30F31E31S33",
-    "F32E32F33E33",
+    "O03O00P03O01P00P01S03O02P02S00S01F03G03g03S02F00",
+    "D03G00P13F01g00D00G01F02P10g01D01S13G02P11g02D02",
+    "S10F13P12Q23S11A23B23O23F10P23S12Q20A20F11B20O20",
+    "Q21A21P20B21O21S23F12P21Q22A22B22S20O22F23P22G23",
+    "S21g23F20D23G20S22g20F21D20P33G21P30g21F22D21G22",
+    "P31g22S33D22P32S30S31S32F30F31F33E30F32E33E31E32",
 )
 
 
@@ -420,7 +427,7 @@
 
     def stage(q):
         gathered(q)
-        hst[...] = hbuf[q].reshape(rows, d)
+        hst[q] = hbuf[q].reshape(rows, d)
 
     def out_product(a, q):
         need("o", "wo")
@@ -432,14 +439,16 @@
 
         d2d(q).start()
 
-    def gate_up(q):
-        stage(q)
-        need("wg", "wu")
-
-        @pl.loop(0, ff // 256)
+    def gate_up(q, half):
+        if half == 0:
+            stage(q)
+            need("wg", "wu")
+        steps_n = ff // 512
+
+        @pl.loop(half * steps_n, (half + 1) * steps_n)
         def _(n):
             cols = pl.ds(pl.multiple_of(n * 256, 256), 256)
-            h = hst[...]
+            h = hst[q]
             g = jnp.dot(h, wg[:, cols], preferred_element_type=F32).astype(BF16).astype(F32)
             u = jnp.dot(h, wu[:, cols], preferred_element_type=F32).astype(BF16).astype(F32)
             abuf[q, :, cols] = (g * jax.nn.sigmoid(g) * u).astype(BF16)
@@ -458,7 +467,7 @@
         stage(q)
         need("wq", "wk", "wv")
         qd, kd = wq.shape[1], wk.shape[1]
-        h = hst[...]
+        h = hst[q]
         qkv_s[q, :, 0:qd] = jnp.dot(h, wq[...], preferred_element_type=F32).astype(BF16)
         qkv_s[q, :, qd:qd + kd] = jnp.dot(h, wk[...], preferred_element_type=F32).astype(BF16)
         qkv_s[q, :, qd + kd:] = jnp.dot(h, wv[...], preferred_element_type=F32).astype(BF16)
@@ -484,7 +493,7 @@
         load(("out", q), hbuf.at[q], x_out.at[q], out_sem.at[q])
 
     steps = [line[i:i + 3] for line in ORDER for i in range(0, len(line), 3)]
-    last = {name: max(i for i, s in enumerate(steps) if s[0] == name and s[1] == "0") for name in "OGD"}
+    last = {name: max(i for i, s in enumerate(steps) if s[0] == name and s[1] == "0") for name in "OgD"}
     for i, code in enumerate(steps):
         name, a, q = code[0], int(code[1]), int(code[2])
         if name == "O":
@@ -495,8 +504,8 @@
             totals(a, q)
         elif name == "F":
             forward(q)
-        elif name == "G":
-            gate_up(q)
+        elif name in "Gg":
+            gate_up(q, "Gg".index(name))
         elif name == "D":
             down(q)
         elif name == "Q":
@@ -509,7 +518,7 @@
             load("wo", wo_hbm.at[1], wo, w_sem.at[0])
             for j in range(kbuf.shape[0] // BLOCK):
                 load_kv(j)
-        if i == last["G"]:
+        if i == last["g"]:
             load("wg", wg_hbm.at[1], wg, w_sem.at[1])
             load("wu", wu_hbm.at[1], wu, w_sem.at[2])
         if i == last["D"]:
@@ -542,7 +551,7 @@
             pltpu.VMEM((CHUNKS, own, d), BF16),
             pltpu.VMEM((CHUNKS, 2, 4, own, d), BF16),
             pltpu.VMEM((CHUNKS, 2, 4, own, d), BF16),
-            pltpu.VMEM((rows, d), BF16),
+            pltpu.VMEM((CHUNKS, rows, d), BF16),
             pltpu.VMEM((CHUNKS, rows, ff), BF16),
             pltpu.VMEM((CHUNKS, rows, qd + 2 * kd), BF16),
             pltpu.VMEM((CHUNKS, 4, own, d), BF16),
@@ -580,7 +589,7 @@
         x = hidden.reshape(CHUNKS, 2, 4, own, d)
         x_out, k_rows, v_rows = body(positions, o, x, mlp_norm, attn_norm, w_out, w_gate, w_up, w_down,
                                      w_query, w_key, w_value, kc, vc, cos2, sin2, posc)
-        k_out, v_out = write_cache(1, positions, k_rows, v_rows, kc, vc, k_out, v_out)
-        return x_out.reshape(batch, d), k_out.reshape(k_cache.shape), v_out.reshape(v_cache.shape)
+        x_out, k_out, v_out = write_cache(1, positions, k_rows, v_rows, x_out.reshape(batch, d), kc, vc, k_out, v_out)
+        return x_out, k_out.reshape(k_cache.shape), v_out.reshape(v_cache.shape)
 
     return jax.shard_map(local_step, mesh=mesh, in_specs=(row_spec, pos_spec, cache_spec, cache_spec, norm_spec, col_spec, col_spec, col_spec, split_rows, norm_spec, col_spec, col_spec, split_rows), out_specs=(row_spec, cache_spec, cache_spec), check_vma=False)

time: 134 us -> 125 us (0.933)
  Pallas kernels: 130 us -> 124 us
  local copies, waits for them, and re-layouts: 2.65 us -> 0 us
    pallas_call x1, Pallas kernels: 96.7 us -> 92.3 us  [body(): pl.pallas_call(body_kernel, in_specs=[pl.BlockSpec(memory_space=pltpu.SME...]
    pallas_call x1, Pallas kernels: 20.7 us -> 17.3 us  [first(): pl.pallas_call(first_kernel, in_specs=[pl.BlockSpec(memory_space=pltpu.SM...]
    unnamed x1 -> x0, local copies, waits for them, and re-layouts: 2.65 us -> none
    pallas_call x1, Pallas kernels: 13 us -> 14.7 us  [write_cache(): pl.pallas_call(functools.partial(cache_kernel, layer), in_specs=[pl.Block...]
where the time goes in v4:
time: 125 us
  Pallas kernels  124 us (99%)
    pallas_call x1, Pallas kernels, body(): pl.pallas_call(body_kernel, in_specs=[pl.BlockSpec(memory_space=pltpu.SME...  92.3 us
    pallas_call x1, Pallas kernels, first(): pl.pallas_call(first_kernel, in_specs=[pl.BlockSpec(memory_space=pltpu.SM...  17.3 us
    pallas_call x1, Pallas kernels, write_cache(): pl.pallas_call(functools.partial(cache_kernel, layer), in_specs=[pl.Block...  14.7 us

profile of v4, /device:TPU:0, one launch (start us, length us, event | category | flops | bytes accessed | tf_op | source)
XLA Modules:
  0.0 125.1 jit_solution(11581924075130889021)
XLA Ops:
  0.6 17.3 %first.1 = (bf16[256,384]{1,0:T(8,128)(2,1)}, f32[256,128]{1,0:T(8,128)}, f32[256,128]{1,0:T(8,128)}, f32[256,128]{1,0:T(8,128)}, bf16[2,256,128,128]{3,2,1,0:T(...) custom-call(s32[256]{0:T(256)} %pos_s.5, bf16[256,3072]{1,0:T(8,128)(2,1)} %x_hbm.1, bf16[2,3072]{1,0:T(2,128)(2,1)} %ga_hbm.1, ...), custom_call_target="tpu_custom_call" | custom-call | tf_op jit(solution)/shard_map/first/pallas_call | solution.py:192
  17.9 92.3 %body.1 = (bf16[4,2,4,8,3072]{4,3,2,1,0:T(8,128)(2,1)}, bf16[256,128]{1,0:T(8,128)(2,1)}, bf16[256,128]{1,0:T(8,128)(2,1)}) custom-call(s32[256]{0:T(256)} %pos_s.5, bf16[256,384]{1,0:T(8,128)(2,1)} %get-tuple-element.15.o_hbm, bf16[4,2,4,8,3072]{4,3,2,1,0:T(8,128)(2,1)} %bitcast.19, bf16[2,3072]{1,0:T(2,128)(2,1)} %gm_hbm.1, bf16[2,3072]{1,0:T(2,128)(2,1)} %ga_hbm.1, ...), custom_call_target="tpu_custom_call" | custom-call | tf_op jit(solution)/shard_map/body/pallas_call | solution.py:541
  110.2 14.7 %write_cache.1 = (bf16[256,3072]{1,0:T(8,128)(2,1)}, bf16[2,256,128,128]{3,2,1,0:T(8,128)(2,1)}, bf16[2,256,128,128]{3,2,1,0:T(8,128)(2,1)}) custom-call(s32[256]{0:T(256)} %pos_s.5, bf16[256,128]{1,0:T(8,128)(2,1)} %get-tuple-element.19.kn_ref, bf16[256,128]{1,0:T(8,128)(2,1)} %get-tuple-element.20.vn_ref, ...), custom_call_target="tpu_custom_call", output_to_operand_aliasing={{1}: (6, {}), {2}: (7, {})} | custom-call | tf_op jit(solution)/shard_map/write_cache/pallas_call | solution.py:266

commit v5 on v4

--- a/solution.py
+++ b/solution.py
@@ -13,7 +13,17 @@
 BF16 = jnp.bfloat16
 MESH = pl.DeviceIdType.MESH
 VMEM_BYTES = 64 * 1024 * 1024 - 128 * 1024
+BODY_BYTES = 36 * 1024 * 1024
+FIRST_BYTES = 48 * 1024 * 1024
 EPS = 1e-5
+
+
+def in_hbm(*arrays):
+    return [pltpu.with_memory_space_constraint(a, pltpu.HBM) for a in arrays]
+
+
+def on_chip(*arrays):
+    return [pltpu.with_memory_space_constraint(a, pltpu.VMEM) for a in arrays]
 
 
 def rope_rows(head_dim):
@@ -70,8 +80,7 @@
         for b8 in range(8):
             b = 8 * j + b8
             k_b = updated(k_at(b), kn[b:b + 1], b)
-            if k_put is not None:
-                k_put(b, k_b)
+            k_put(b, k_b)
             s_b = lax.dot_general(qj, k_b, (((1,), (1,)), ((), ())), preferred_element_type=F32)
             scores = s_b if scores is None else jnp.where(row_of == b8, s_b, scores)
         all_scores.append(scores)
@@ -89,19 +98,18 @@
         for b8 in range(8):
             b = 8 * j + b8
             v_b = updated(v_at(b), vn[b:b + 1], b)
-            if v_put is not None:
-                v_put(b, v_b)
+            v_put(b, v_b)
             o_b = jnp.dot(probs[j], v_b, preferred_element_type=F32)
             mixed = o_b if mixed is None else jnp.where(row_of == b8, o_b, mixed)
         outs.append(mixed)
     o = [jnp.concatenate([m[8 * h:8 * h + 8] for m in outs], axis=0).astype(BF16) for h in range(heads)]
-    return o, kn, vn
+    return o
 
 
 def first_kernel(
-    pos_s, x_hbm, g_hbm, wq_hbm, wk_hbm, wv_hbm, pos_ref, rope_ref, k_hbm, v_hbm,
-    o_ref, cos_ref, sin_ref, posc_ref, ko_hbm, vo_hbm,
-    h_ref, g_ref, wq, wk, wv, qkv_ref, kbuf, vbuf, sem, in_sem, out_sem,
+    pos_hbm, x_hbm, g_hbm, wq_hbm, wk_hbm, wv_hbm, wo_hbm, pos2_hbm, rope_hbm, k_hbm, v_hbm,
+    o_ref, wo_ref, cos_ref, sin_ref, posc_ref, ko_hbm, vo_hbm,
+    h_ref, g_ref, wq, wk, wv, pos_s, pos_ref, rope_ref, qkv_ref, kbuf, vbuf, sem, in_sem, out_sem,
 ):
     rows = h_ref.shape[0]
     qd = wq.shape[1]
@@ -109,7 +117,9 @@
     blocks = rows // BLOCK
     copies = [pltpu.make_async_copy(src, dst, sem.at[i]) for i, (src, dst) in enumerate(
         [(x_hbm, h_ref), (g_hbm, g_ref), (wq_hbm.at[0], wq), (wk_hbm.at[0], wk), (wv_hbm.at[0], wv)])]
-    for cp in copies:
+    small = [pltpu.make_async_copy(src, dst, sem.at[i]) for i, (src, dst) in enumerate(
+        [(pos_hbm, pos_s), (pos2_hbm, pos_ref), (rope_hbm, rope_ref)], 6)]
+    for cp in copies[:2] + small + copies[2:]:
         cp.start()
 
     def reads(i):
@@ -122,6 +132,8 @@
         return (pltpu.make_async_copy(kbuf.at[at], ko_hbm.at[0, at], out_sem.at[0, i]),
                 pltpu.make_async_copy(vbuf.at[at], vo_hbm.at[0, at], out_sem.at[1, i]))
 
+    for cp in small:
+        cp.wait()
     width = pos_ref.shape[1]
     diagonal = (lax.broadcasted_iota(jnp.int32, (width, width), 0) == lax.broadcasted_iota(jnp.int32, (width, width), 1))
     for i in range(rows // width):
@@ -138,6 +150,8 @@
     for i in range(blocks):
         for cp in reads(i):
             cp.start()
+    wo_copy = pltpu.make_async_copy(wo_hbm.at[0], wo_ref, sem.at[5])
+    wo_copy.start()
     gain = g_ref[0:1, :].astype(F32)
 
     @pl.loop(0, rows // 16)
@@ -166,7 +180,7 @@
         def v_put(b, value):
             vbuf[base + b] = value
 
-        o, _, _ = attend_block(
+        o = attend_block(
             qkv_ref[at, :], cos_ref[at, :], sin_ref[at, :], posc_ref[at, :], lambda b: pos_s[base + b],
             lambda b: kbuf[base + b], lambda b: vbuf[base + b], k_put, v_put)
         for n, o_n in enumerate(o):
@@ -177,9 +191,10 @@
     for i in range(blocks):
         for cp in writes(i):
             cp.wait()
-
-
-def first(hidden, attn_norm, w_query, w_key, w_value, positions, k_cache, v_cache):
+    wo_copy.wait()
+
+
+def first(hidden, attn_norm, w_query, w_key, w_value, w_out, positions, k_cache, v_cache):
     rows, d = hidden.shape
     qd, kd = w_query.shape[2], w_key.shape[2]
     seq = k_cache.shape[2]
@@ -187,93 +202,57 @@
     vmem = pl.BlockSpec(memory_space=pltpu.VMEM)
     hbm = pl.BlockSpec(memory_space=pl.ANY)
     dma = pltpu.SemaphoreType.DMA
-    table = jax.ShapeDtypeStruct((rows, kd), F32)
+    table = pltpu.VMEM((rows, kd), F32)
     cache = jax.ShapeDtypeStruct(k_cache.shape, BF16)
     return pl.pallas_call(
         first_kernel,
-        in_specs=[pl.BlockSpec(memory_space=pltpu.SMEM)] + [hbm] * 5 + [vmem, vmem, hbm, hbm],
-        out_specs=[vmem] * 4 + [hbm, hbm],
-        out_shape=[jax.ShapeDtypeStruct((rows, qd), BF16), table, table, table, cache, cache],
+        in_specs=[hbm] * 11,
+        out_specs=[vmem] * 5 + [hbm, hbm],
+        out_shape=[pltpu.VMEM((rows, qd), BF16), pltpu.VMEM(w_out.shape[1:], BF16), table, table, table, cache, cache],
         scratch_shapes=[
             pltpu.VMEM((rows, d), BF16), pltpu.VMEM(attn_norm.shape, BF16), pltpu.VMEM((d, qd), BF16),
-            pltpu.VMEM((d, kd), BF16), pltpu.VMEM((d, kd), BF16), pltpu.VMEM((rows, qd + 2 * kd), BF16),
+            pltpu.VMEM((d, kd), BF16), pltpu.VMEM((d, kd), BF16),
+            pltpu.SMEM((rows,), jnp.int32), pltpu.VMEM((rows // kd, kd), jnp.int32), pltpu.VMEM((2, kd), F32),
+            pltpu.VMEM((rows, qd + 2 * kd), BF16),
             pltpu.VMEM((rows, seq, kd), BF16), pltpu.VMEM((rows, seq, kd), BF16),
-            dma((5,)), dma((2, blocks)), dma((2, blocks)),
+            dma((9,)), dma((2, blocks)), dma((2, blocks)),
         ],
-        compiler_params=pltpu.CompilerParams(vmem_limit_bytes=VMEM_BYTES),
+        compiler_params=pltpu.CompilerParams(vmem_limit_bytes=FIRST_BYTES),
         name="first",
-    )(positions, hidden, attn_norm, w_query, w_key, w_value, positions.reshape(rows // kd, kd),
-      jnp.asarray(rope_rows(kd)), k_cache, v_cache)
-
-
-def cache_kernel(
-    layer, pos_s, kn_ref, vn_ref, x_hbm, k_hbm, v_hbm, k_prev, v_prev,
-    x_out, ko_hbm, vo_hbm,
-    kbuf, vbuf, xbuf, in_sem, out_sem, x_sem,
-):
-    batch, seq, head = kbuf.shape
+    )(*in_hbm(positions, hidden, attn_norm, w_query, w_key, w_value, w_out, positions.reshape(rows // kd, kd),
+              jnp.asarray(rope_rows(kd)), k_cache, v_cache))
+
+
+def cache_kernel(layer, x_ref, k_ref, v_ref, k_prev, v_prev, x_hbm, ko_hbm, vo_hbm, out_sem, x_sem):
+    batch = k_ref.shape[0]
     blocks = batch // BLOCK
-    x_in = pltpu.make_async_copy(x_hbm, xbuf, x_sem.at[0])
-    x_in.start()
-    x_put = pltpu.make_async_copy(xbuf, x_out, x_sem.at[1])
-
-    def reads(i):
+    writes = []
+    for i in range(blocks):
         at = pl.ds(i * BLOCK, BLOCK)
-        return (pltpu.make_async_copy(k_hbm.at[layer, at], kbuf.at[at], in_sem.at[0, i]),
-                pltpu.make_async_copy(v_hbm.at[layer, at], vbuf.at[at], in_sem.at[1, i]))
-
-    def writes(i):
-        at = pl.ds(i * BLOCK, BLOCK)
-        return (pltpu.make_async_copy(kbuf.at[at], ko_hbm.at[layer, at], out_sem.at[0, i]),
-                pltpu.make_async_copy(vbuf.at[at], vo_hbm.at[layer, at], out_sem.at[1, i]))
-
-    for i in range(blocks):
-        for cp in reads(i):
-            cp.start()
-    row_of = lax.broadcasted_iota(jnp.int32, (16, head), 0)
-
-    @pl.loop(0, blocks)
-    def _(i):
-        base = pl.multiple_of(i * BLOCK, BLOCK)
-        at = pl.ds(base, BLOCK)
-        new_rows = [(ref[at, :].astype(F32), buf) for ref, buf in ((kn_ref, kbuf), (vn_ref, vbuf))]
-        for cp in reads(i):
-            cp.wait()
-        for b in range(BLOCK):
-            pos = pos_s[base + b]
-            tile = pl.ds(pl.multiple_of(pos // 16 * 16, 16), 16)
-            here = row_of == pos % 16
-            for rows, buf in new_rows:
-                old = buf[base + b, tile, :].astype(F32)
-                buf[base + b, tile, :] = jnp.where(here, rows[b:b + 1], old).astype(BF16)
-        for cp in writes(i):
-            cp.start()
-
-    x_in.wait()
-    x_put.start()
-    for i in range(blocks):
-        for cp in writes(i):
-            cp.wait()
-    x_put.wait()
-
-
-def write_cache(layer, positions, k_rows, v_rows, x, k_cache, v_cache, k_prev, v_prev):
-    layers, batch, seq, head = k_cache.shape
-    blocks = batch // BLOCK
+        writes.append(pltpu.make_async_copy(k_ref.at[at], ko_hbm.at[layer, at], out_sem.at[0, i]))
+        writes.append(pltpu.make_async_copy(v_ref.at[at], vo_hbm.at[layer, at], out_sem.at[1, i]))
+    writes.append(pltpu.make_async_copy(x_ref, x_hbm, x_sem.at[0]))
+    for cp in writes:
+        cp.start()
+    for cp in writes:
+        cp.wait()
+
+
+def write_cache(layer, x, k_layer, v_layer, k_prev, v_prev):
+    blocks = k_layer.shape[0] // BLOCK
     vmem = pl.BlockSpec(memory_space=pltpu.VMEM)
     hbm = pl.BlockSpec(memory_space=pl.ANY)
     dma = pltpu.SemaphoreType.DMA
     return pl.pallas_call(
         functools.partial(cache_kernel, layer),
-        in_specs=[pl.BlockSpec(memory_space=pltpu.SMEM), vmem, vmem] + [hbm] * 5,
+        in_specs=[vmem, vmem, vmem, hbm, hbm],
         out_specs=[hbm] * 3,
-        out_shape=[jax.ShapeDtypeStruct(a.shape, BF16) for a in (x, k_cache, v_cache)],
-        input_output_aliases={6: 1, 7: 2},
-        scratch_shapes=[pltpu.VMEM((batch, seq, head), BF16), pltpu.VMEM((batch, seq, head), BF16), pltpu.VMEM(x.shape, BF16),
-                        dma((2, blocks)), dma((2, blocks)), dma((2,))],
-        compiler_params=pltpu.CompilerParams(vmem_limit_bytes=VMEM_BYTES),
+        out_shape=[jax.ShapeDtypeStruct(a.shape, BF16) for a in (x, k_prev, v_prev)],
+        input_output_aliases={3: 1, 4: 2},
+        scratch_shapes=[dma((2, blocks)), dma((1,))],
+        compiler_params=pltpu.CompilerParams(vmem_limit_bytes=2 * 1024 * 1024),
         name="write_cache",
-    )(positions, k_rows, v_rows, x, k_cache, v_cache, k_prev, v_prev)
+    )(x, k_layer, v_layer, k_prev, v_prev)
 
 
 CHUNKS = 4
@@ -289,12 +268,11 @@
 
 
 def body_kernel(
-    pos_s, o_hbm, x_hbm, gm_hbm, ga_hbm, wo_hbm, wg_hbm, wu_hbm, wd_hbm, wq_hbm, wk_hbm, wv_hbm, k_hbm, v_hbm,
-    cos_hbm, sin_hbm, posc_hbm,
-    x_out, kn_out, vn_out,
-    wo, wg, wu, wd, wq, wk, wv, kbuf, vbuf, o_s, xres, part, hbuf, hst, abuf, qkv_s, d2d_in, rs_out, rs_in, acc,
-    gm, ga, cos, sin, posc,
-    w_sem, x_sem, kv_sem, t_sem, out_sem, d2d_s, d2d_r, rs_s, rs_r, ag_s, ag_r, fw_s, fw_r,
+    o_first, wo_first, cos, sin, posc, pos_hbm, x_hbm, gm_hbm, ga_hbm, wo_hbm, wg_hbm, wu_hbm, wd_hbm, wq_hbm, wk_hbm, wv_hbm, k_hbm, v_hbm,
+    x_out, kbuf, vbuf,
+    wo, wg, wu, wd, wq, wk, wv, o_s, xres, part, hbuf, hst, abuf, qkv_s, d2d_in, rs_out, rs_in, acc,
+    gm, ga, pos_s,
+    w_sem, x_sem, kv_sem, t_sem, d2d_s, d2d_r, rs_s, rs_r, ag_s, ag_r, fw_s, fw_r,
 ):
     chunks, _, _, own, d = part.shape
     rows = 8 * own
@@ -320,21 +298,18 @@
             if name in loads:
                 loads.pop(name).wait()
 
-    load("o", o_hbm, o_s, t_sem.at[0])
-    load("wo", wo_hbm.at[0], wo, w_sem.at[0])
-    load("gm", gm_hbm, gm, t_sem.at[1])
+    load("gm", gm_hbm, gm, t_sem.at[0])
     for q in range(chunks):
         load(("x", q), x_hbm.at[q, core, chip], xres.at[q], x_sem.at[q])
     load("wg", wg_hbm.at[0], wg, w_sem.at[1])
     load("wu", wu_hbm.at[0], wu, w_sem.at[2])
     load("wd", wd_hbm.at[0], wd, w_sem.at[3])
-    load("ga", ga_hbm, ga, t_sem.at[2])
+    load("ga", ga_hbm, ga, t_sem.at[1])
+    load("pos", pos_hbm, pos_s, t_sem.at[2])
     load("wq", wq_hbm.at[1], wq, w_sem.at[4])
     load("wk", wk_hbm.at[1], wk, w_sem.at[5])
     load("wv", wv_hbm.at[1], wv, w_sem.at[6])
-    load("cos", cos_hbm, cos, t_sem.at[3])
-    load("sin", sin_hbm, sin, t_sem.at[4])
-    load("posc", posc_hbm, posc, t_sem.at[5])
+    load("wo", wo_hbm.at[1], wo, w_sem.at[0])
 
     def load_kv(i):
         at = pl.ds(i * BLOCK, BLOCK)
@@ -430,12 +405,14 @@
         hst[q] = hbuf[q].reshape(rows, d)
 
     def out_product(a, q):
-        need("o", "wo")
+        if a:
+            need("wo")
+        o, w = (o_s, wo) if a else (o_first, wo_first)
 
         @pl.loop(0, d // 1024)
         def _(n):
             cols = pl.ds(pl.multiple_of(n * 1024, 1024), 1024)
-            put_part(q, cols, jnp.dot(o_s[q * rows:(q + 1) * rows, :], wo[:, cols], preferred_element_type=F32))
+            put_part(q, cols, jnp.dot(o[q * rows:(q + 1) * rows, :], w[:, cols], preferred_element_type=F32))
 
         d2d(q).start()
 
@@ -473,24 +450,29 @@
         qkv_s[q, :, qd + kd:] = jnp.dot(h, wv[...], preferred_element_type=F32).astype(BF16)
 
     def attend(q, i):
-        need("cos", "sin", "posc")
         for j in range(rows // BLOCK // 2):
+            need("pos")
             first = i * (rows // 2) + j * BLOCK
             block = (q * rows + first) // BLOCK
             need(("k", block), ("v", block))
             base = block * BLOCK
             at = slice(base, base + BLOCK)
-            o, kn, vn = attend_block(
+
+            def k_put(b, value):
+                kbuf[base + b] = value
+
+            def v_put(b, value):
+                vbuf[base + b] = value
+
+            o = attend_block(
                 qkv_s[q, first:first + BLOCK, :], cos[at, :], sin[at, :], posc[at, :], lambda b: pos_s[base + b],
-                lambda b: kbuf[base + b], lambda b: vbuf[base + b], None, None)
+                lambda b: kbuf[base + b], lambda b: vbuf[base + b], k_put, v_put)
             for h, o_h in enumerate(o):
                 o_s[at, h * head:(h + 1) * head] = o_h
-            kn_out[at, :] = kn.astype(BF16)
-            vn_out[at, :] = vn.astype(BF16)
 
     def result(q):
         gathered(q)
-        load(("out", q), hbuf.at[q], x_out.at[q], out_sem.at[q])
+        x_out[q] = hbuf[q]
 
     steps = [line[i:i + 3] for line in ORDER for i in range(0, len(line), 3)]
     last = {name: max(i for i, s in enumerate(steps) if s[0] == name and s[1] == "0") for name in "OgD"}
@@ -515,7 +497,6 @@
         else:
             result(q)
         if i == last["O"]:
-            load("wo", wo_hbm.at[1], wo, w_sem.at[0])
             for j in range(kbuf.shape[0] // BLOCK):
                 load_kv(j)
         if i == last["g"]:
@@ -523,10 +504,9 @@
             load("wu", wu_hbm.at[1], wu, w_sem.at[2])
         if i == last["D"]:
             load("wd", wd_hbm.at[1], wd, w_sem.at[3])
-    need(*[("out", q) for q in range(chunks)])
-
-
-def body(positions, o, x, mlp_norm, attn_norm, w_out, w_gate, w_up, w_down, w_query, w_key, w_value, k_cache, v_cache, cos2, sin2, posc):
+
+
+def body(positions, o, wo_first, x, mlp_norm, attn_norm, w_out, w_gate, w_up, w_down, w_query, w_key, w_value, k_cache, v_cache, cos2, sin2, posc):
     batch, qd = o.shape
     d = w_out.shape[2]
     ff = w_gate.shape[2]
@@ -537,16 +517,15 @@
     vmem = pl.BlockSpec(memory_space=pltpu.VMEM)
     hbm = pl.BlockSpec(memory_space=pl.ANY)
     dma = pltpu.SemaphoreType.DMA
-    row = jax.ShapeDtypeStruct((batch, kd), BF16)
+    cache = pltpu.VMEM((batch, seq, kd), BF16)
     return pl.pallas_call(
         body_kernel,
-        in_specs=[pl.BlockSpec(memory_space=pltpu.SMEM)] + [hbm] * 16,
-        out_specs=[hbm, vmem, vmem],
-        out_shape=[jax.ShapeDtypeStruct((CHUNKS, 2, 4, own, d), BF16), row, row],
+        in_specs=[vmem] * 5 + [hbm] * 13,
+        out_specs=[vmem] * 3,
+        out_shape=[pltpu.VMEM((CHUNKS, 2, 4, own, d), BF16), cache, cache],
         scratch_shapes=[
             pltpu.VMEM((qd, d), BF16), pltpu.VMEM((d, ff), BF16), pltpu.VMEM((d, ff), BF16), pltpu.VMEM((ff, d), BF16),
             pltpu.VMEM((d, qd), BF16), pltpu.VMEM((d, kd), BF16), pltpu.VMEM((d, kd), BF16),
-            pltpu.VMEM((batch, seq, kd), BF16), pltpu.VMEM((batch, seq, kd), BF16),
             pltpu.VMEM((batch, qd), BF16),
             pltpu.VMEM((CHUNKS, own, d), BF16),
             pltpu.VMEM((CHUNKS, 2, 4, own, d), BF16),
@@ -558,17 +537,17 @@
             pltpu.VMEM((CHUNKS, 3, own, d), BF16),
             pltpu.VMEM((CHUNKS, 3, own, d), BF16),
             pltpu.VMEM((CHUNKS, own, d), F32),
-            pltpu.VMEM(mlp_norm.shape, BF16), pltpu.VMEM(attn_norm.shape, BF16),
-            pltpu.VMEM((batch, kd), F32), pltpu.VMEM((batch, kd), F32), pltpu.VMEM((batch, kd), F32),
-            dma((7,)), dma((CHUNKS,)), dma((2, batch // BLOCK)), dma((6,)), dma((CHUNKS,)),
+            pltpu.VMEM(mlp_norm.shape, BF16), pltpu.VMEM(attn_norm.shape, BF16), pltpu.SMEM((batch,), jnp.int32),
+            dma((7,)), dma((CHUNKS,)), dma((2, batch // BLOCK)), dma((3,)),
             dma((CHUNKS,)), dma((CHUNKS,)),
             dma((CHUNKS, 3)), dma((CHUNKS, 3)),
             dma((CHUNKS, 3)), dma((CHUNKS, 3)),
             dma((CHUNKS, 4)), dma((CHUNKS, 4)),
         ],
-        compiler_params=pltpu.CompilerParams(vmem_limit_bytes=VMEM_BYTES, collective_id=0, has_side_effects=True),
+        compiler_params=pltpu.CompilerParams(vmem_limit_bytes=BODY_BYTES, collective_id=0, has_side_effects=True),
         name="body",
-    )(positions, o, x, mlp_norm, attn_norm, w_out, w_gate, w_up, w_down, w_query, w_key, w_value, k_cache, v_cache, cos2, sin2, posc)
+    )(*on_chip(o, wo_first, cos2, sin2, posc),
+      *in_hbm(positions, x, mlp_norm, attn_norm, w_out, w_gate, w_up, w_down, w_query, w_key, w_value, k_cache, v_cache))
 
 
 def solution(mesh):
@@ -585,11 +564,11 @@
         own = batch // (8 * CHUNKS)
         kc = k_cache.reshape(layers, batch, seq, head)
         vc = v_cache.reshape(layers, batch, seq, head)
-        o, cos2, sin2, posc, k_out, v_out = first(hidden, attn_norm, w_query, w_key, w_value, positions, kc, vc)
+        o, wo_first, cos2, sin2, posc, k_out, v_out = first(hidden, attn_norm, w_query, w_key, w_value, w_out, positions, kc, vc)
         x = hidden.reshape(CHUNKS, 2, 4, own, d)
-        x_out, k_rows, v_rows = body(positions, o, x, mlp_norm, attn_norm, w_out, w_gate, w_up, w_down,
+        x_out, k_layer, v_layer = body(positions, o, wo_first, x, mlp_norm, attn_norm, w_out, w_gate, w_up, w_down,
                                      w_query, w_key, w_value, kc, vc, cos2, sin2, posc)
-        x_out, k_out, v_out = write_cache(1, positions, k_rows, v_rows, x_out.reshape(batch, d), kc, vc, k_out, v_out)
+        x_out, k_out, v_out = write_cache(1, x_out.reshape(batch, d), k_layer, v_layer, k_out, v_out)
         return x_out, k_out.reshape(k_cache.shape), v_out.reshape(v_cache.shape)
 
     return jax.shard_map(local_step, mesh=mesh, in_specs=(row_spec, pos_spec, cache_spec, cache_spec, norm_spec, col_spec, col_spec, col_spec, split_rows, norm_spec, col_spec, col_spec, split_rows), out_specs=(row_spec, cache_spec, cache_spec), check_vma=False)

time: 125 us -> 112 us (0.90)
  Pallas kernels: 124 us -> 111 us
    pallas_call x3, Pallas kernels: 124 us -> 111 us  [the longest x1 88.8 us: body(): pl.pallas_call(body_kernel, in_specs=[vmem] * 5 + [hbm] * 13, out_specs=[...]
where the time goes in v5:
time: 112 us
  Pallas kernels  111 us (99%)
    pallas_call x1, Pallas kernels, body(): pl.pallas_call(body_kernel, in_specs=[vmem] * 5 + [hbm] * 13, out_specs=[...  88.8 us
    pallas_call x1, Pallas kernels, first(): pl.pallas_call(first_kernel, in_specs=[hbm] * 11, out_specs=[vmem] * 5 +...  16.1 us
    pallas_call x1, Pallas kernels, write_cache(): pl.pallas_call(functools.partial(cache_kernel, layer), in_specs=[vmem, vm...  6.46 us

profile of v5, /device:TPU:0, one launch (start us, length us, event | category | flops | bytes accessed | tf_op | source)
XLA Modules:
  0.0 112.2 jit_solution(3984167988579205845)
XLA Ops:
  0.6 16.1 %first.1 = (bf16[256,384]{1,0:T(8,128)(2,1)S(1)}, bf16[384,3072]{1,0:T(8,128)(2,1)S(1)}, f32[256,128]{1,0:T(8,128)S(1)}, f32[256,128]{1,0:T(8,128)S(1)}, f32[256...) custom-call(s32[256]{0:T(256)} %pos_hbm.3, bf16[256,3072]{1,0:T(8,128)(2,1)} %x_hbm.1, ...), custom_call_target="tpu_custom_call" | custom-call | tf_op jit(solution)/shard_map/first/pallas_call | solution.py:207
  16.7 88.8 %body.1 = (bf16[4,2,4,8,3072]{4,3,2,1,0:T(8,128)(2,1)S(1)}, bf16[256,128,128]{2,1,0:T(8,128)(2,1)S(1)}, bf16[256,128,128]{2,1,0:T(8,128)(2,1)S(1)}) custom-call(bf16[256,384]{1,0:T(8,128)(2,1)S(1)} %get-tuple-element.16.o_first, bf16[384,3072]{1,0:T(8,128)(2,1)S(1)} %get-tuple-element.17.wo_first, f32[256,128]{1,0:T(8,128)S(1)} %get-tuple-element.18.cos, ...), custom_call_target="tpu_custom_call" | custom-call | tf_op jit(solution)/shard_map/body/pallas_call | solution.py:521
  105.5 6.5 %write_cache.1 = (bf16[256,3072]{1,0:T(8,128)(2,1)}, bf16[2,256,128,128]{3,2,1,0:T(8,128)(2,1)}, bf16[2,256,128,128]{3,2,1,0:T(8,128)(2,1)}) custom-call(bf16[256,3072]{1,0:T(8,128)(2,1)S(1)} %bitcast.11, bf16[256,128,128]{2,1,0:T(8,128)(2,1)S(1)} %get-tuple-element.22.k_ref, ...), custom_call_target="tpu_custom_call", output_to_operand_aliasing={{1}: (3, {}), {2}: (4, {})} | custom-call | tf_op jit(solution)/shard_map/write_cache/pallas_call | solution.py:246

commit v6 on v5

--- a/solution.py
+++ b/solution.py
@@ -13,9 +13,12 @@
 BF16 = jnp.bfloat16
 MESH = pl.DeviceIdType.MESH
 VMEM_BYTES = 64 * 1024 * 1024 - 128 * 1024
-BODY_BYTES = 36 * 1024 * 1024
-FIRST_BYTES = 48 * 1024 * 1024
+BODY_BYTES = 34 * 1024 * 1024
+FIRST_BYTES = 24 * 1024 * 1024
 EPS = 1e-5
+CHUNKS = 4
+EARLY = 2
+COLS = 1024
 
 
 def in_hbm(*arrays):
@@ -108,13 +111,13 @@
 
 def first_kernel(
     pos_hbm, x_hbm, g_hbm, wq_hbm, wk_hbm, wv_hbm, wo_hbm, pos2_hbm, rope_hbm, k_hbm, v_hbm,
-    o_ref, wo_ref, cos_ref, sin_ref, posc_ref, ko_hbm, vo_hbm,
-    h_ref, g_ref, wq, wk, wv, pos_s, pos_ref, rope_ref, qkv_ref, kbuf, vbuf, sem, in_sem, out_sem,
+    o_ref, wo_ref, cos_ref, sin_ref, posc_ref, qkv_ref, ko_hbm, vo_hbm,
+    h_ref, g_ref, wq, wk, wv, pos_s, pos_ref, rope_ref, kbuf, vbuf, sem, in_sem, out_sem,
 ):
     rows = h_ref.shape[0]
     qd = wq.shape[1]
     kd = wk.shape[1]
-    blocks = rows // BLOCK
+    blocks = kbuf.shape[0] // BLOCK
     copies = [pltpu.make_async_copy(src, dst, sem.at[i]) for i, (src, dst) in enumerate(
         [(x_hbm, h_ref), (g_hbm, g_ref), (wq_hbm.at[0], wq), (wk_hbm.at[0], wk), (wv_hbm.at[0], wv)])]
     small = [pltpu.make_async_copy(src, dst, sem.at[i]) for i, (src, dst) in enumerate(
@@ -198,7 +201,8 @@
     rows, d = hidden.shape
     qd, kd = w_query.shape[2], w_key.shape[2]
     seq = k_cache.shape[2]
-    blocks = rows // BLOCK
+    head_rows = EARLY * (rows // CHUNKS)
+    blocks = head_rows // BLOCK
     vmem = pl.BlockSpec(memory_space=pltpu.VMEM)
     hbm = pl.BlockSpec(memory_space=pl.ANY)
     dma = pltpu.SemaphoreType.DMA
@@ -207,14 +211,14 @@
     return pl.pallas_call(
         first_kernel,
         in_specs=[hbm] * 11,
-        out_specs=[vmem] * 5 + [hbm, hbm],
-        out_shape=[pltpu.VMEM((rows, qd), BF16), pltpu.VMEM(w_out.shape[1:], BF16), table, table, table, cache, cache],
+        out_specs=[vmem] * 6 + [hbm, hbm],
+        out_shape=[pltpu.VMEM((head_rows, qd), BF16), pltpu.VMEM(w_out.shape[1:], BF16), table, table, table,
+                   pltpu.VMEM((rows, qd + 2 * kd), BF16), cache, cache],
         scratch_shapes=[
             pltpu.VMEM((rows, d), BF16), pltpu.VMEM(attn_norm.shape, BF16), pltpu.VMEM((d, qd), BF16),
             pltpu.VMEM((d, kd), BF16), pltpu.VMEM((d, kd), BF16),
             pltpu.SMEM((rows,), jnp.int32), pltpu.VMEM((rows // kd, kd), jnp.int32), pltpu.VMEM((2, kd), F32),
-            pltpu.VMEM((rows, qd + 2 * kd), BF16),
-            pltpu.VMEM((rows, seq, kd), BF16), pltpu.VMEM((rows, seq, kd), BF16),
+            pltpu.VMEM((head_rows, seq, kd), BF16), pltpu.VMEM((head_rows, seq, kd), BF16),
             dma((9,)), dma((2, blocks)), dma((2, blocks)),
         ],
         compiler_params=pltpu.CompilerParams(vmem_limit_bytes=FIRST_BYTES),
@@ -223,53 +227,52 @@
               jnp.asarray(rope_rows(kd)), k_cache, v_cache))
 
 
-def cache_kernel(layer, x_ref, k_ref, v_ref, k_prev, v_prev, x_hbm, ko_hbm, vo_hbm, out_sem, x_sem):
+def cache_kernel(x_ref, k_ref, v_ref, k0_ref, v0_ref, k_prev, v_prev, x_hbm, ko_hbm, vo_hbm, out_sem, x_sem):
     batch = k_ref.shape[0]
-    blocks = batch // BLOCK
-    writes = []
-    for i in range(blocks):
-        at = pl.ds(i * BLOCK, BLOCK)
-        writes.append(pltpu.make_async_copy(k_ref.at[at], ko_hbm.at[layer, at], out_sem.at[0, i]))
-        writes.append(pltpu.make_async_copy(v_ref.at[at], vo_hbm.at[layer, at], out_sem.at[1, i]))
-    writes.append(pltpu.make_async_copy(x_ref, x_hbm, x_sem.at[0]))
+    late = k0_ref.shape[0]
+    jobs = [(src, dst, 1, i, i) for i in range(0, batch, BLOCK) for src, dst in ((k_ref, ko_hbm), (v_ref, vo_hbm))]
+    jobs += [(src, dst, 0, i, batch - late + i) for i in range(0, late, BLOCK)
+             for src, dst in ((k0_ref, ko_hbm), (v0_ref, vo_hbm))]
+    writes = [pltpu.make_async_copy(x_ref, x_hbm, x_sem.at[0])]
+    for n, (src, dst, layer, i, o) in enumerate(jobs):
+        writes.append(pltpu.make_async_copy(src.at[pl.ds(i, BLOCK)], dst.at[layer, pl.ds(o, BLOCK)], out_sem.at[n]))
     for cp in writes:
         cp.start()
     for cp in writes:
         cp.wait()
 
 
-def write_cache(layer, x, k_layer, v_layer, k_prev, v_prev):
-    blocks = k_layer.shape[0] // BLOCK
+def write_cache(x, k_layer, v_layer, k_late, v_late, k_prev, v_prev):
+    blocks = (k_layer.shape[0] + k_late.shape[0]) // BLOCK
     vmem = pl.BlockSpec(memory_space=pltpu.VMEM)
     hbm = pl.BlockSpec(memory_space=pl.ANY)
     dma = pltpu.SemaphoreType.DMA
     return pl.pallas_call(
-        functools.partial(cache_kernel, layer),
-        in_specs=[vmem, vmem, vmem, hbm, hbm],
+        cache_kernel,
+        in_specs=[vmem] * 5 + [hbm, hbm],
         out_specs=[hbm] * 3,
         out_shape=[jax.ShapeDtypeStruct(a.shape, BF16) for a in (x, k_prev, v_prev)],
-        input_output_aliases={3: 1, 4: 2},
-        scratch_shapes=[dma((2, blocks)), dma((1,))],
+        input_output_aliases={5: 1, 6: 2},
+        scratch_shapes=[dma((2 * blocks,)), dma((1,))],
         compiler_params=pltpu.CompilerParams(vmem_limit_bytes=2 * 1024 * 1024),
         name="write_cache",
-    )(x, k_layer, v_layer, k_prev, v_prev)
-
-
-CHUNKS = 4
+    )(x, k_layer, v_layer, k_late, v_late, k_prev, v_prev)
+
 
 ORDER = (
-    "O03O00P03O01P00P01S03O02P02S00S01F03G03g03S02F00",
-    "D03G00P13F01g00D00G01F02P10g01D01S13G02P11g02D02",
-    "S10F13P12Q23S11A23B23O23F10P23S12Q20A20F11B20O20",
-    "Q21A21P20B21O21S23F12P21Q22A22B22S20O22F23P22G23",
-    "S21g23F20D23G20S22g20F21D20P33G21P30g21F22D21G22",
-    "P31g22S33D22P32S30S31S32F30F31F33E30F32E33E31E32",
+    "O00O01P00A03P01B03O03A02P03B02O02S00P02S03S01F00",
+    "G00g00S02D00F03P10G03F01g03D03G01P13g01F02S10D01",
+    "G02P11g02S13D02F10P12Q20A20S11B20O20F13P20Q23A23",
+    "S12B23O23F11P23Q21A21B21S20O21F12P21Q22A22S23B22",
+    "O22F20P22G20S21g20F23D20G23S22g23P30F21D23G21P33",
+    "g21F22D21G22P31S30g22D22P32S31S33F30S32F31E30F33",
+    "E33F32E31E32",
 )
 
 
 def body_kernel(
-    o_first, wo_first, cos, sin, posc, pos_hbm, x_hbm, gm_hbm, ga_hbm, wo_hbm, wg_hbm, wu_hbm, wd_hbm, wq_hbm, wk_hbm, wv_hbm, k_hbm, v_hbm,
-    x_out, kbuf, vbuf,
+    o_first, wo_first, cos, sin, posc, qkv_first, pos_hbm, x_hbm, gm_hbm, ga_hbm, wo_hbm, wg_hbm, wu_hbm, wd_hbm, wq_hbm, wk_hbm, wv_hbm, k_hbm, v_hbm,
+    x_out, kbuf, vbuf, kbuf0, vbuf0,
     wo, wg, wu, wd, wq, wk, wv, o_s, xres, part, hbuf, hst, abuf, qkv_s, d2d_in, rs_out, rs_in, acc,
     gm, ga, pos_s,
     w_sem, x_sem, kv_sem, t_sem, d2d_s, d2d_r, rs_s, rs_r, ag_s, ag_r, fw_s, fw_r,
@@ -298,24 +301,33 @@
             if name in loads:
                 loads.pop(name).wait()
 
+    load("pos", pos_hbm, pos_s, t_sem.at[2])
     load("gm", gm_hbm, gm, t_sem.at[0])
+    early = kbuf.shape[0] - kbuf0.shape[0]
+
+    def load_kv(layer, i):
+        at = pl.ds(i * BLOCK, BLOCK)
+        if layer:
+            k_to, v_to = kbuf.at[at], vbuf.at[at]
+        else:
+            at0 = pl.ds(i * BLOCK - early, BLOCK)
+            k_to, v_to = kbuf0.at[at0], vbuf0.at[at0]
+        load(("k", layer, i), k_hbm.at[layer, at], k_to, kv_sem.at[2 * layer, i])
+        load(("v", layer, i), v_hbm.at[layer, at], v_to, kv_sem.at[2 * layer + 1, i])
+
+    for i in range(early // BLOCK, kbuf.shape[0] // BLOCK):
+        load_kv(0, i)
     for q in range(chunks):
         load(("x", q), x_hbm.at[q, core, chip], xres.at[q], x_sem.at[q])
     load("wg", wg_hbm.at[0], wg, w_sem.at[1])
     load("wu", wu_hbm.at[0], wu, w_sem.at[2])
     load("wd", wd_hbm.at[0], wd, w_sem.at[3])
     load("ga", ga_hbm, ga, t_sem.at[1])
-    load("pos", pos_hbm, pos_s, t_sem.at[2])
     load("wq", wq_hbm.at[1], wq, w_sem.at[4])
     load("wk", wk_hbm.at[1], wk, w_sem.at[5])
     load("wv", wv_hbm.at[1], wv, w_sem.at[6])
     load("wo", wo_hbm.at[1], wo, w_sem.at[0])
 
-    def load_kv(i):
-        at = pl.ds(i * BLOCK, BLOCK)
-        load(("k", i), k_hbm.at[1, at], kbuf.at[at], kv_sem.at[0, i])
-        load(("v", i), v_hbm.at[1, at], vbuf.at[at], kv_sem.at[1, i])
-
     barrier = pltpu.get_barrier_semaphore()
     for dev in [partner] + peers[1:]:
         pl.semaphore_signal(barrier, inc=1, device_id=dev, device_id_type=MESH)
@@ -325,8 +337,9 @@
         return pltpu.make_async_remote_copy(
             src_ref=src, dst_ref=dst, send_sem=s, recv_sem=r, device_id=dev, device_id_type=MESH)
 
-    def d2d(q):
-        return remote(part.at[q, 1 - core], d2d_in.at[q], d2d_s.at[q], d2d_r.at[q], partner)
+    def d2d(q, n):
+        cols = pl.ds(pl.multiple_of(n * COLS, COLS), COLS)
+        return remote(part.at[q, 1 - core, :, :, cols], d2d_in.at[q, :, :, cols], d2d_s.at[q, n], d2d_r.at[q, n], partner)
 
     def rs(q, k):
         return remote(rs_out.at[q, k - 1], rs_in.at[q, k - 1], rs_s.at[q, k - 1], rs_r.at[q, k - 1], peers[k])
@@ -354,13 +367,15 @@
                 part[q, p, c, :, cols] = value[at:at + own].astype(BF16)
 
     def pair_sums(q):
-        d2d(q).wait_recv()
+        for n in range(d // COLS):
+            d2d(q, n).wait_recv()
         for k in order:
             pair = part[q, core, chips[k]].astype(F32) + d2d_in[q, chips[k]].astype(F32)
             rs_out[q, k - 1] = pair.astype(BF16)
             rs(q, k).start()
         acc[q] = part[q, core, chip].astype(F32) + d2d_in[q, chip].astype(F32)
-        d2d(q).wait_send()
+        for n in range(d // COLS):
+            d2d(q, n).wait_send()
 
     def totals(a, q):
         for k in (1, 2, 3):
@@ -407,14 +422,14 @@
     def out_product(a, q):
         if a:
             need("wo")
-        o, w = (o_s, wo) if a else (o_first, wo_first)
-
-        @pl.loop(0, d // 1024)
+        o = o_first if a == 0 and q < EARLY else o_s
+        w = wo if a else wo_first
+
+        @pl.loop(0, d // COLS)
         def _(n):
-            cols = pl.ds(pl.multiple_of(n * 1024, 1024), 1024)
+            cols = pl.ds(pl.multiple_of(n * COLS, COLS), COLS)
             put_part(q, cols, jnp.dot(o[q * rows:(q + 1) * rows, :], w[:, cols], preferred_element_type=F32))
-
-        d2d(q).start()
+            d2d(q, n).start()
 
     def gate_up(q, half):
         if half == 0:
@@ -433,12 +448,11 @@
     def down(q):
         need("wd")
 
-        @pl.loop(0, d // 1024)
+        @pl.loop(0, d // COLS)
         def _(n):
-            cols = pl.ds(pl.multiple_of(n * 1024, 1024), 1024)
+            cols = pl.ds(pl.multiple_of(n * COLS, COLS), COLS)
             put_part(q, cols, jnp.dot(abuf[q], wd[:, cols], preferred_element_type=F32))
-
-        d2d(q).start()
+            d2d(q, n).start()
 
     def qkv(q):
         stage(q)
@@ -449,24 +463,26 @@
         qkv_s[q, :, qd:qd + kd] = jnp.dot(h, wk[...], preferred_element_type=F32).astype(BF16)
         qkv_s[q, :, qd + kd:] = jnp.dot(h, wv[...], preferred_element_type=F32).astype(BF16)
 
-    def attend(q, i):
-        for j in range(rows // BLOCK // 2):
-            need("pos")
-            first = i * (rows // 2) + j * BLOCK
-            block = (q * rows + first) // BLOCK
-            need(("k", block), ("v", block))
-            base = block * BLOCK
+    def attend(a, q, i):
+        need("pos")
+        source, k_ref, v_ref, offset = (qkv_s.at[q], kbuf, vbuf, 0) if a else (qkv_first, kbuf0, vbuf0, early)
+        half = rows // 2
+        for j in range(half // BLOCK):
+            base = q * rows + i * half + j * BLOCK
+            block = base // BLOCK
+            need(("k", a // 2, block), ("v", a // 2, block))
             at = slice(base, base + BLOCK)
+            first_row = base - q * rows if a else base
 
             def k_put(b, value):
-                kbuf[base + b] = value
+                k_ref[base - offset + b] = value
 
             def v_put(b, value):
-                vbuf[base + b] = value
+                v_ref[base - offset + b] = value
 
             o = attend_block(
-                qkv_s[q, first:first + BLOCK, :], cos[at, :], sin[at, :], posc[at, :], lambda b: pos_s[base + b],
-                lambda b: kbuf[base + b], lambda b: vbuf[base + b], k_put, v_put)
+                source[first_row:first_row + BLOCK, :], cos[at, :], sin[at, :], posc[at, :], lambda b: pos_s[base + b],
+                lambda b: k_ref[base - offset + b], lambda b: v_ref[base - offset + b], k_put, v_put)
             for h, o_h in enumerate(o):
                 o_s[at, h * head:(h + 1) * head] = o_h
 
@@ -493,12 +509,12 @@
         elif name == "Q":
             qkv(q)
         elif name in "AB":
-            attend(q, "AB".index(name))
+            attend(a, q, "AB".index(name))
         else:
             result(q)
         if i == last["O"]:
             for j in range(kbuf.shape[0] // BLOCK):
-                load_kv(j)
+                load_kv(1, j)
         if i == last["g"]:
             load("wg", wg_hbm.at[1], wg, w_sem.at[1])
             load("wu", wu_hbm.at[1], wu, w_sem.at[2])
@@ -506,23 +522,23 @@
             load("wd", wd_hbm.at[1], wd, w_sem.at[3])
 
 
-def body(positions, o, wo_first, x, mlp_norm, attn_norm, w_out, w_gate, w_up, w_down, w_query, w_key, w_value, k_cache, v_cache, cos2, sin2, posc):
-    batch, qd = o.shape
+def body(positions, o, wo_first, x, mlp_norm, attn_norm, w_out, w_gate, w_up, w_down, w_query, w_key, w_value, k_cache, v_cache, tables, qkv):
+    batch, seq, kd = k_cache.shape[1:]
+    qd = o.shape[1]
     d = w_out.shape[2]
     ff = w_gate.shape[2]
-    kd = w_key.shape[2]
-    seq = k_cache.shape[2]
     own = batch // (8 * CHUNKS)
     rows = 8 * own
     vmem = pl.BlockSpec(memory_space=pltpu.VMEM)
     hbm = pl.BlockSpec(memory_space=pl.ANY)
     dma = pltpu.SemaphoreType.DMA
     cache = pltpu.VMEM((batch, seq, kd), BF16)
+    late = pltpu.VMEM((batch - o.shape[0], seq, kd), BF16)
     return pl.pallas_call(
         body_kernel,
-        in_specs=[vmem] * 5 + [hbm] * 13,
-        out_specs=[vmem] * 3,
-        out_shape=[pltpu.VMEM((CHUNKS, 2, 4, own, d), BF16), cache, cache],
+        in_specs=[vmem] * 6 + [hbm] * 13,
+        out_specs=[vmem] * 5,
+        out_shape=[pltpu.VMEM((CHUNKS, 2, 4, own, d), BF16), cache, cache, late, late],
         scratch_shapes=[
             pltpu.VMEM((qd, d), BF16), pltpu.VMEM((d, ff), BF16), pltpu.VMEM((d, ff), BF16), pltpu.VMEM((ff, d), BF16),
             pltpu.VMEM((d, qd), BF16), pltpu.VMEM((d, kd), BF16), pltpu.VMEM((d, kd), BF16),
@@ -538,15 +554,15 @@
             pltpu.VMEM((CHUNKS, 3, own, d), BF16),
             pltpu.VMEM((CHUNKS, own, d), F32),
             pltpu.VMEM(mlp_norm.shape, BF16), pltpu.VMEM(attn_norm.shape, BF16), pltpu.SMEM((batch,), jnp.int32),
-            dma((7,)), dma((CHUNKS,)), dma((2, batch // BLOCK)), dma((3,)),
-            dma((CHUNKS,)), dma((CHUNKS,)),
+            dma((7,)), dma((CHUNKS,)), dma((4, batch // BLOCK)), dma((3,)),
+            dma((CHUNKS, d // COLS)), dma((CHUNKS, d // COLS)),
             dma((CHUNKS, 3)), dma((CHUNKS, 3)),
             dma((CHUNKS, 3)), dma((CHUNKS, 3)),
             dma((CHUNKS, 4)), dma((CHUNKS, 4)),
         ],
         compiler_params=pltpu.CompilerParams(vmem_limit_bytes=BODY_BYTES, collective_id=0, has_side_effects=True),
         name="body",
-    )(*on_chip(o, wo_first, cos2, sin2, posc),
+    )(*on_chip(o, wo_first, *tables, qkv),
       *in_hbm(positions, x, mlp_norm, attn_norm, w_out, w_gate, w_up, w_down, w_query, w_key, w_value, k_cache, v_cache))
 
 
@@ -564,11 +580,11 @@
         own = batch // (8 * CHUNKS)
         kc = k_cache.reshape(layers, batch, seq, head)
         vc = v_cache.reshape(layers, batch, seq, head)
-        o, wo_first, cos2, sin2, posc, k_out, v_out = first(hidden, attn_norm, w_query, w_key, w_value, w_out, positions, kc, vc)
+        o, wo_first, *tables, qkv, k_out, v_out = first(hidden, attn_norm, w_query, w_key, w_value, w_out, positions, kc, vc)
         x = hidden.reshape(CHUNKS, 2, 4, own, d)
-        x_out, k_layer, v_layer = body(positions, o, wo_first, x, mlp_norm, attn_norm, w_out, w_gate, w_up, w_down,
-                                     w_query, w_key, w_value, kc, vc, cos2, sin2, posc)
-        x_out, k_out, v_out = write_cache(1, x_out.reshape(batch, d), k_layer, v_layer, k_out, v_out)
+        x_out, *caches = body(positions, o, wo_first, x, mlp_norm, attn_norm, w_out, w_gate, w_up, w_down,
+                              w_query, w_key, w_value, kc, vc, tables, qkv)
+        x_out, k_out, v_out = write_cache(x_out.reshape(batch, d), *caches, k_out, v_out)
         return x_out, k_out.reshape(k_cache.shape), v_out.reshape(v_cache.shape)
 
     return jax.shard_map(local_step, mesh=mesh, in_specs=(row_spec, pos_spec, cache_spec, cache_spec, norm_spec, col_spec, col_spec, col_spec, split_rows, norm_spec, col_spec, col_spec, split_rows), out_specs=(row_spec, cache_spec, cache_spec), check_vma=False)

time: 112 us -> 118 us (1.054)
  Pallas kernels: 111 us -> 117 us
    pallas_call x3, Pallas kernels: 111 us -> 117 us  [the longest x1 96.5 us: body(): pl.pallas_call(body_kernel, in_specs=[vmem] * 6 + [hbm] * 13, out_specs=[...]
where the time goes in v6:
time: 118 us
  Pallas kernels  117 us (99%)
    pallas_call x1, Pallas kernels, body(): pl.pallas_call(body_kernel, in_specs=[vmem] * 6 + [hbm] * 13, out_specs=[...  96.5 us
    pallas_call x1, Pallas kernels, first(): pl.pallas_call(first_kernel, in_specs=[hbm] * 11, out_specs=[vmem] * 6 +...  11.6 us
    pallas_call x1, Pallas kernels, write_cache(): pl.pallas_call(cache_kernel, in_specs=[vmem] * 5 + [hbm, hbm], out_specs=...  9.04 us

profile of v6, /device:TPU:0, one launch (start us, length us, event | category | flops | bytes accessed | tf_op | source)
XLA Modules:
  0.0 117.9 jit_solution(11501519337525686139)
XLA Ops:
  0.6 11.6 %first.1 = (bf16[128,384]{1,0:T(8,128)(2,1)S(1)}, bf16[384,3072]{1,0:T(8,128)(2,1)S(1)}, f32[256,128]{1,0:T(8,128)S(1)}, f32[256,128]{1,0:T(8,128)S(1)}, f32[256...) custom-call(s32[256]{0:T(256)} %pos_hbm.3, ...), custom_call_target="tpu_custom_call" | custom-call | tf_op jit(solution)/shard_map/first/pallas_call | solution.py:211
  12.2 96.5 %body.1 = (bf16[4,2,4,8,3072]{4,3,2,1,0:T(8,128)(2,1)S(1)}, bf16[256,128,128]{2,1,0:T(8,128)(2,1)S(1)}, bf16[256,128,128]{2,1,0:T(8,128)(2,1)S(1)}, bf16[128,128...) custom-call(bf16[128,384]{1,0:T(8,128)(2,1)S(1)} %get-tuple-element.19.o_first, ...), custom_call_target="tpu_custom_call" | custom-call | tf_op jit(solution)/shard_map/body/pallas_call | solution.py:537
  108.7 9.0 %write_cache.1 = (bf16[256,3072]{1,0:T(8,128)(2,1)}, bf16[2,256,128,128]{3,2,1,0:T(8,128)(2,1)}, bf16[2,256,128,128]{3,2,1,0:T(8,128)(2,1)}) custom-call(bf16[256,3072]{1,0:T(8,128)(2,1)S(1)} %bitcast.11, bf16[256,128,128]{2,1,0:T(8,128)(2,1)S(1)} %get-tuple-element.26.k_ref, ...), custom_call_target="tpu_custom_call", output_to_operand_aliasing={{1}: (5, {}), {2}: (6, {})} | custom-call | tf_op jit(solution)/shard_map/write_cache/pallas_call | solution.py:250

commit v7 on v6

--- a/solution.py
+++ b/solution.py
@@ -315,18 +315,13 @@
         load(("k", layer, i), k_hbm.at[layer, at], k_to, kv_sem.at[2 * layer, i])
         load(("v", layer, i), v_hbm.at[layer, at], v_to, kv_sem.at[2 * layer + 1, i])
 
-    for i in range(early // BLOCK, kbuf.shape[0] // BLOCK):
-        load_kv(0, i)
+    steps = [line[i:i + 3] for line in ORDER for i in range(0, len(line), 3)]
+    for code in steps:
+        if code[0] in "AB" and code[1] == "0":
+            load_kv(0, (int(code[2]) * rows + "AB".index(code[0]) * rows // 2) // BLOCK)
     for q in range(chunks):
         load(("x", q), x_hbm.at[q, core, chip], xres.at[q], x_sem.at[q])
-    load("wg", wg_hbm.at[0], wg, w_sem.at[1])
-    load("wu", wu_hbm.at[0], wu, w_sem.at[2])
-    load("wd", wd_hbm.at[0], wd, w_sem.at[3])
     load("ga", ga_hbm, ga, t_sem.at[1])
-    load("wq", wq_hbm.at[1], wq, w_sem.at[4])
-    load("wk", wk_hbm.at[1], wk, w_sem.at[5])
-    load("wv", wv_hbm.at[1], wv, w_sem.at[6])
-    load("wo", wo_hbm.at[1], wo, w_sem.at[0])
 
     barrier = pltpu.get_barrier_semaphore()
     for dev in [partner] + peers[1:]:
@@ -490,8 +485,8 @@
         gathered(q)
         x_out[q] = hbuf[q]
 
-    steps = [line[i:i + 3] for line in ORDER for i in range(0, len(line), 3)]
     last = {name: max(i for i, s in enumerate(steps) if s[0] == name and s[1] == "0") for name in "OgD"}
+    first_at = {name: min(i for i, s in enumerate(steps) if s[0] == name) for name in "AGD"}
     for i, code in enumerate(steps):
         name, a, q = code[0], int(code[1]), int(code[2])
         if name == "O":
@@ -512,7 +507,17 @@
             attend(a, q, "AB".index(name))
         else:
             result(q)
+        if i == first_at["A"]:
+            load("wg", wg_hbm.at[0], wg, w_sem.at[1])
+            load("wu", wu_hbm.at[0], wu, w_sem.at[2])
         if i == last["O"]:
+            load("wd", wd_hbm.at[0], wd, w_sem.at[3])
+        if i == first_at["G"]:
+            load("wq", wq_hbm.at[1], wq, w_sem.at[4])
+            load("wk", wk_hbm.at[1], wk, w_sem.at[5])
+            load("wv", wv_hbm.at[1], wv, w_sem.at[6])
+            load("wo", wo_hbm.at[1], wo, w_sem.at[0])
+        if i == first_at["D"]:
             for j in range(kbuf.shape[0] // BLOCK):
                 load_kv(1, j)
         if i == last["g"]:

time: 118 us -> 113 us (0.958)
  Pallas kernels: 117 us -> 112 us
    pallas_call x1, Pallas kernels: 96.5 us -> 91.2 us  [body(): pl.pallas_call(body_kernel, in_specs=[vmem] * 6 + [hbm] * 13, out_specs=[...]
where the time goes in v7:
time: 113 us
  Pallas kernels  112 us (99%)
    pallas_call x1, Pallas kernels, body(): pl.pallas_call(body_kernel, in_specs=[vmem] * 6 + [hbm] * 13, out_specs=[...  91.2 us
    pallas_call x1, Pallas kernels, first(): pl.pallas_call(first_kernel, in_specs=[hbm] * 11, out_specs=[vmem] * 6 +...  11.6 us
    pallas_call x1, Pallas kernels, write_cache(): pl.pallas_call(cache_kernel, in_specs=[vmem] * 5 + [hbm, hbm], out_specs=...  9.04 us

profile of v7, /device:TPU:0, one launch (start us, length us, event | category | flops | bytes accessed | tf_op | source)
XLA Modules:
  0.0 112.6 jit_solution(16408397248752298649)
XLA Ops:
  0.6 11.6 %first.1 = (bf16[128,384]{1,0:T(8,128)(2,1)S(1)}, bf16[384,3072]{1,0:T(8,128)(2,1)S(1)}, f32[256,128]{1,0:T(8,128)S(1)}, f32[256,128]{1,0:T(8,128)S(1)}, f32[256...) custom-call(s32[256]{0:T(256)} %pos_hbm.3, ...), custom_call_target="tpu_custom_call" | custom-call | tf_op jit(solution)/shard_map/first/pallas_call | solution.py:211
  12.2 91.2 %body.1 = (bf16[4,2,4,8,3072]{4,3,2,1,0:T(8,128)(2,1)S(1)}, bf16[256,128,128]{2,1,0:T(8,128)(2,1)S(1)}, bf16[256,128,128]{2,1,0:T(8,128)(2,1)S(1)}, bf16[128,128...) custom-call(bf16[128,384]{1,0:T(8,128)(2,1)S(1)} %get-tuple-element.19.o_first, ...), custom_call_target="tpu_custom_call" | custom-call | tf_op jit(solution)/shard_map/body/pallas_call | solution.py:542
  103.4 9.0 %write_cache.1 = (bf16[256,3072]{1,0:T(8,128)(2,1)}, bf16[2,256,128,128]{3,2,1,0:T(8,128)(2,1)}, bf16[2,256,128,128]{3,2,1,0:T(8,128)(2,1)}) custom-call(bf16[256,3072]{1,0:T(8,128)(2,1)S(1)} %bitcast.11, bf16[256,128,128]{2,1,0:T(8,128)(2,1)S(1)} %get-tuple-element.26.k_ref, ...), custom_call_target="tpu_custom_call", output_to_operand_aliasing={{1}: (5, {}), {2}: (6, {})} | custom-call | tf_op jit(solution)/shard_map/write_cache/pallas_call | solution.py:250

commit v8 on v5

--- a/solution.py
+++ b/solution.py
@@ -496,7 +496,7 @@
             attend(q, "AB".index(name))
         else:
             result(q)
-        if i == last["O"]:
+        if code == "D00":
             for j in range(kbuf.shape[0] // BLOCK):
                 load_kv(j)
         if i == last["g"]:

time: 112 us -> 112 us (level)
  no operation moved by 1% of the time
where the time goes in v8:
time: 112 us
  Pallas kernels  111 us (99%)
    pallas_call x1, Pallas kernels, body(): pl.pallas_call(body_kernel, in_specs=[vmem] * 5 + [hbm] * 13, out_specs=[...  88.8 us
    pallas_call x1, Pallas kernels, first(): pl.pallas_call(first_kernel, in_specs=[hbm] * 11, out_specs=[vmem] * 5 +...  16.1 us
    pallas_call x1, Pallas kernels, write_cache(): pl.pallas_call(functools.partial(cache_kernel, layer), in_specs=[vmem, vm...  6.46 us

profile of v8, /device:TPU:0, one launch (start us, length us, event | category | flops | bytes accessed | tf_op | source)
XLA Modules:
  0.0 112.2 jit_solution(15814515608801009790)
XLA Ops:
  0.6 16.1 %first.1 = (bf16[256,384]{1,0:T(8,128)(2,1)S(1)}, bf16[384,3072]{1,0:T(8,128)(2,1)S(1)}, f32[256,128]{1,0:T(8,128)S(1)}, f32[256,128]{1,0:T(8,128)S(1)}, f32[256...) custom-call(s32[256]{0:T(256)} %pos_hbm.3, bf16[256,3072]{1,0:T(8,128)(2,1)} %x_hbm.1, ...), custom_call_target="tpu_custom_call" | custom-call | tf_op jit(solution)/shard_map/first/pallas_call | solution.py:207
  16.7 88.8 %body.1 = (bf16[4,2,4,8,3072]{4,3,2,1,0:T(8,128)(2,1)S(1)}, bf16[256,128,128]{2,1,0:T(8,128)(2,1)S(1)}, bf16[256,128,128]{2,1,0:T(8,128)(2,1)S(1)}) custom-call(bf16[256,384]{1,0:T(8,128)(2,1)S(1)} %get-tuple-element.16.o_first, bf16[384,3072]{1,0:T(8,128)(2,1)S(1)} %get-tuple-element.17.wo_first, f32[256,128]{1,0:T(8,128)S(1)} %get-tuple-element.18.cos, ...), custom_call_target="tpu_custom_call" | custom-call | tf_op jit(solution)/shard_map/body/pallas_call | solution.py:521
  105.5 6.5 %write_cache.1 = (bf16[256,3072]{1,0:T(8,128)(2,1)}, bf16[2,256,128,128]{3,2,1,0:T(8,128)(2,1)}, bf16[2,256,128,128]{3,2,1,0:T(8,128)(2,1)}) custom-call(bf16[256,3072]{1,0:T(8,128)(2,1)S(1)} %bitcast.11, bf16[256,128,128]{2,1,0:T(8,128)(2,1)S(1)} %get-tuple-element.22.k_ref, ...), custom_call_target="tpu_custom_call", output_to_operand_aliasing={{1}: (3, {}), {2}: (4, {})} | custom-call | tf_op jit(solution)/shard_map/write_cache/pallas_call | solution.py:246
